TPU v7x, 32 devices: a whole 2x2x4 slice. The times are simulated.
32 devices in a mesh: tok: 16 (over z, y, core), tp: 2 (over x).
Axes of the slice: x: 2, y: 2, z: 4, core: 2. Of those that a mesh axis runs over, the one named last changes fastest.
Arguments:
- hidden: bfloat16 [1536, 8192], P('tok'), may hold values from -2600 to 2600
- norm_gain: float32 [8192], replicated, may hold values from 0.5 to 1.5
- w_query: bfloat16 [8192, 4096], P('tok', 'tp'), may hold values from -1 to 1
- w_key: bfloat16 [8192, 1024], P('tok', 'tp'), may hold values from -1 to 1
- w_value: bfloat16 [8192, 1024], P('tok', 'tp'), may hold values from -0.0625 to 0.0625
- doc_ids: int32 [1536], P('tok'), may hold values from 0 to 3, as said below
Outputs:
- attended: bfloat16 [1536, 4096], P('tok', 'tp')
- out_scale: float32 [4096], P('tp')
- folded_gain: float32 [8192], P(('tok', 'tp'))
- codes_query: float32 [8192, 4096], P(('tok', 'tp'))
- codes_key: float32 [8192, 1024], P(('tok', 'tp'))
- codes_value: float32 [8192, 1024], P(('tok', 'tp'))
- scale_query: float32 [4096], P('tp')
- scale_key: float32 [1024], P('tp')
- scale_value: float32 [1024], P('tp')
Inputs may be any that keep to these rules, and one draw needn't show every extreme that they name: doc_ids never falls along the tokens; each of the 4 documents holds 1 to 1152 tokens and one holds exactly 1152.
All inputs are finite; a program needn't handle non-finite values. Where the computation divides by a largest or mean magnitude, that divisor is 1e-20 or more.
Results may differ from a plain program's by a relative error of at most 0.005.
The roundings to bfloat16 on the way count: a program that leaves them out, or rounds other values in their place, can miss the bound.
Values may be sent and summed in bfloat16 or wider, within the bound.
A program may use at most 128 MiB of HBM per device.

v0:
```python
import math

import jax
import jax.numpy as jnp
from jax import lax
from jax.sharding import PartitionSpec as P

HEAD = 128
KVH = 8
QHEADS = 32


def rotate(states, positions):
    half = states.shape[-1] // 2
    inverse = jnp.exp(
        jnp.arange(half, dtype=jnp.float32) * (-2.0 * math.log(10000.0) / states.shape[-1])
    )
    angles = positions[:, None] * inverse[None, :]
    cosine = jnp.cos(angles)[:, None, :]
    sine = jnp.sin(angles)[:, None, :]
    first = states[..., :half]
    second = states[..., half:]
    return jnp.concatenate(
        [first * cosine - second * sine, second * cosine + first * sine], axis=-1
    )


def smooth_from(input_peak, weight_peak):
    return jnp.sqrt(jnp.maximum(input_peak, 1e-05)) / jnp.sqrt(jnp.maximum(weight_peak, 1e-05))


def on_device(hidden, norm_gain, w_query, w_key, w_value, doc_ids):
    tok_dev = hidden.shape[0]
    row_count = w_query.shape[0]
    tp_count = lax.axis_size("tp")
    tok_index = lax.axis_index("tok")
    tp_index = lax.axis_index("tp")
    heads_here = w_query.shape[1] // HEAD
    kv_here = w_key.shape[1] // HEAD
    group_size = QHEADS // KVH
    matrices = (w_query, w_key, w_value)
    states = hidden.astype(jnp.float32)
    normed = (
        states
        * lax.rsqrt(jnp.mean(states * states, axis=1, keepdims=True) + 1e-05)
        * norm_gain[None, :]
    ).astype(jnp.bfloat16)
    input_peak = lax.pmax(
        jnp.max(jnp.abs(normed), axis=0).astype(jnp.float32).astype(jnp.bfloat16), "tok"
    ).astype(jnp.float32)
    relaid = (
        lax.all_to_all(w_query, "tp", split_axis=0, concat_axis=1, tiled=True),
        lax.all_to_all(w_key, "tp", split_axis=0, concat_axis=1, tiled=True),
        lax.all_to_all(w_value, "tp", split_axis=0, concat_axis=1, tiled=True),
    )
    pieces = (
        lax.all_gather(w_query, "tok", axis=0, tiled=True),
        lax.all_gather(w_key, "tok", axis=0, tiled=True),
        lax.all_gather(w_value, "tok", axis=0, tiled=True),
    )
    projected = tuple(
        (jnp.dot(normed, piece, preferred_element_type=jnp.float32) for piece in pieces)
    )
    local_peak = jnp.max(
        jnp.stack([jnp.max(jnp.abs(matrix), axis=1) for matrix in matrices]), axis=0
    ).astype(jnp.float32)
    row_peak = lax.pmax(local_peak, "tp")
    input_rows = lax.dynamic_slice_in_dim(input_peak, tok_index * row_count, row_count)
    smoothing_rows = smooth_from(input_rows, row_peak)
    column_local = tuple(
        (
            jnp.max(jnp.abs(smoothing_rows[:, None] * matrix.astype(jnp.float32)), axis=0)
            for matrix in matrices
        )
    )
    column_global = lax.pmax(column_local, "tok")
    scales = tuple((jnp.maximum(column, 1e-05) / 127.0 for column in column_global))
    query_positions = tok_index * tok_dev + jnp.arange(tok_dev, dtype=jnp.int32)
    positions = query_positions.astype(jnp.float32)
    query = (
        rotate(projected[0].reshape(tok_dev, heads_here, HEAD), positions)
        .astype(jnp.bfloat16)
        .reshape(tok_dev, kv_here, group_size, HEAD)
    )
    key = (
        rotate(projected[1].reshape(tok_dev, kv_here, HEAD), positions)
        .astype(jnp.bfloat16)
        .reshape(tok_dev, kv_here * HEAD)
    )
    value = projected[2].astype(jnp.bfloat16)
    score_scale = 1.0 / math.sqrt(HEAD)
    highest = jnp.full((kv_here, group_size, tok_dev), -1e30, jnp.float32)
    key_block = lax.all_gather(key, "tok", axis=0, tiled=True)
    value_block = lax.all_gather(value, "tok", axis=0, tiled=True)
    doc_block = lax.all_gather(doc_ids, "tok", axis=0, tiled=True)
    length = key_block.shape[0]
    scores = (
        jnp.einsum(
            "tkgd,skd->kgts",
            query,
            key_block.reshape(length, kv_here, HEAD),
            preferred_element_type=jnp.float32,
        )
        * score_scale
    )
    key_positions = jnp.arange(length, dtype=jnp.int32)
    allowed = (doc_ids[:, None] == doc_block[None, :]) & (
        key_positions[None, :] <= query_positions[:, None]
    )
    scores = jnp.where(allowed, scores, -1e30)
    raised = jnp.maximum(highest, jnp.max(scores, axis=3))
    weights = jnp.where(allowed, jnp.exp(scores - raised[..., None]), 0.0)
    totals = jnp.sum(weights, axis=3)
    accumulated = jnp.einsum(
        "kgts,skd->kgtd",
        weights.astype(jnp.bfloat16),
        value_block.reshape(length, kv_here, HEAD),
        preferred_element_type=jnp.float32,
    )
    highest, totals, accumulated = (raised, totals, accumulated)
    attended = (
        (accumulated / totals[..., None])
        .transpose(2, 0, 1, 3)
        .reshape(tok_dev, heads_here * HEAD)
        .astype(jnp.bfloat16)
    )
    out_scale = lax.pmax(jnp.max(jnp.abs(attended), axis=0).astype(jnp.float32), "tok")
    sub_rows = row_count // tp_count
    smooth_part = lax.dynamic_slice_in_dim(smoothing_rows, tp_index * sub_rows, sub_rows)
    gain_part = lax.dynamic_slice_in_dim(
        norm_gain, tok_index * row_count + tp_index * sub_rows, sub_rows
    )
    folded_gain = gain_part / smooth_part
    every_scale = lax.all_gather(scales, "tp", axis=0, tiled=True)
    codes = tuple(
        (
            smooth_part[:, None] * block.astype(jnp.float32) / column_scale[None, :]
            for block, column_scale in zip(relaid, every_scale)
        )
    )
    return (
        attended,
        out_scale,
        folded_gain,
        codes[0],
        codes[1],
        codes[2],
        scales[0],
        scales[1],
        scales[2],
    )


def solution(mesh):
    in_specs = (P("tok", None), P(), P("tok", "tp"), P("tok", "tp"), P("tok", "tp"), P("tok"))
    out_specs = (
        P("tok", "tp"),
        P("tp"),
        P(("tok", "tp")),
        P(("tok", "tp"), None),
        P(("tok", "tp"), None),
        P(("tok", "tp"), None),
        P("tp"),
        P("tp"),
        P("tp"),
    )
    return jax.shard_map(
        on_device, mesh=mesh, in_specs=in_specs, out_specs=out_specs, check_vma=False
    )
```

profile of v0, /device:TPU:0, one launch (start us, length us, event | category | flops | bytes accessed | tf_op | source)
XLA Modules:
  0.0 528.4 jit_solution(10473979587659237486)
XLA Ops:
  10.9 76.4 %all-gather.8.cloned.1.call-done = bf16[8192,512]{1,0:T(8,128)(2,1)} async-done(((bf16[512,512]{1,0:T(8,128)(2,1)}), bf16[8192,512]{1,0:T(8,128)(2,1)}) %all-gather.8.cloned.1.call-update) | async-done | bytes 8388624 | tf_op jit(solution)/shard_map/all_gather | solution.py:58
  87.2 4.9 fusion.40
  93.3 69.0 %all-gather.14.cloned.1.call-done = bf16[8192,512]{1,0:T(8,128)(2,1)} async-done(((bf16[512,512]{1,0:T(8,128)(2,1)}), bf16[8192,512]{1,0:T(8,128)(2,1)}) %all-gather.14.cloned.1.call-update) | async-done | bytes 8388624 | tf_op jit(solution)/shard_map/all_gather | solution.py:59
  162.3 5.5 %convolution_convert_fusion = bf16[96,512]{1,0:T(8,128)(2,1)} fusion(bf16[8192,512]{1,0:T(8,128)(2,1)} %all-gather.14.cloned.1.call-done, bf16[96,8192]{1,0:T(8,128)(2,1)S(1)} %copy-done, f32[8192]{0:T(1024)S(1)} %copy-done.3, f32[96]{0:T(128)S(1)} %add_rsqrt_fusion), kind=kOutput, calls=%fused_computation.20 | convolution fusion | flops 808501248 | bytes 10092928 | tf_op jit(solution)/shard_map/dot_general | solution.py:62
  168.4 3.5 all-to-all-start.1
  177.0 3.6 all-to-all-done.1
  180.6 3.5 all-to-all-start.2
  184.1 8.0 %pmax.44 = f32[512]{0:T(512)S(1)} all-reduce(f32[512]{0:T(512)S(1)} %maximum_convert_fusion), channel_id=1, replica_groups=mesh['tok'=16,'tp'=2] {'tp'}, use_global_device_ids=true, to_apply=%region_10.0 | all-reduce | flops 512 | bytes 4096 | tf_op jit(solution)/shard_map/pmax | solution.py:67
  192.1 57.9 %pmax.43 = bf16[8192]{0:T(1024)(128)(2,1)S(1)} all-reduce(bf16[8192]{0:T(1024)(128)(2,1)S(1)} %abs_reduce_fusion.2), channel_id=1, replica_groups=mesh['tok'=16,'tp'=2] {'tok'}, use_global_device_ids=true, to_apply=%region_6.0 | all-reduce | flops 8192 | bytes 32768 | tf_op jit(solution)/shard_map/pmax | solution.py:48
  250.0 4.9 all-to-all-start
  256.5 7.9 %all-reduce = s32[1536]{0:T(1024)S(1)} all-reduce(s32[1536]{0:T(1024)S(1)} %dynamic-update-slice), channel_id=1, replica_groups=mesh['tok'=16,'tp'=2] {'tok'}, use_global_device_ids=true, to_apply=%add | all-reduce | flops 1536 | bytes 12288
  271.2 4.5 all-to-all-done
  275.8 3.9 copy.42
  281.4 3.5 reshape.143
  285.0 127.6 %all-gather.12.cloned.1.call-done = bf16[8192,2048]{1,0:T(8,128)(2,1)} async-done(((bf16[512,2048]{1,0:T(8,128)(2,1)}), bf16[8192,2048]{1,0:T(8,128)(2,1)}) %all-gather.12.cloned.1.call-update) | async-done | bytes 33554448 | tf_op jit(solution)/shard_map/all_gather | solution.py:57
  412.6 13.4 %convolution_bitcast_fusion = f32[12,8,16,128]{3,1,2,0:T(8,128)S(1)} fusion(bf16[8192,2048]{1,0:T(8,128)(2,1)} %all-gather.12.cloned.1.call-done, bf16[96,8192]{1,0:T(8,128)(2,1)S(1)} %copy-done, f32[8192]{0:T(1024)S(1)} %copy-done.3, f32[96]{0:T(128)S(1)} %add_rsqrt_fusion), kind=kOutput, calls=%fused_computation.19 | convolution fusion | flops 3224371200 | bytes 35946880 | tf_op jit(solution)/shard_map/dot_general | solution.py:62
  428.8 2.8 fusion.1
  431.6 3.2 abs_reduce_fusion.7
  434.7 60.6 %all-reduce.1 = (f32[2048]{0:T(1024)}, f32[2048]{0:T(1024)S(1)}, f32[512]{0:T(512)S(1)}, f32[512]{0:T(512)S(1)}) all-reduce(bf16[2048]{0:T(1024)(128)(2,1)S(1)} %bitcast.86, f32[2048]{0:T(1024)S(1)} %abs_reduce_fusion, f32[512]{0:T(512)S(1)} %get-tuple-element.19, f32[512]{0:T(512)S(1)} %get-tuple-element.18), channel_id=1, replica_groups=mesh['tok'=16,'tp'=2] {'tok'}, use_global_device_ids=true, to_apply=%region_4.0 | all-reduce | flops 5120 | bytes 36864 | tf_op jit(solution)/shard_map/pmax | solution.py:127
  495.4 4.4 all-gather
  499.8 4.4 all-gather.1
  507.1 4.4 all_gather.33
  511.5 3.5 fusion.6
  515.0 5.6 %copy.45 = f32[256,4096]{1,0:T(8,128)} copy(f32[256,4096]{0,1:T(8,128)} %fusion.6) | data formatting | bytes 8388608
  (75 shorter events, 26.7 us)
Async XLA Ops:
  7.2 80.0 %copy-start = (bf16[96,8192]{1,0:T(8,128)(2,1)S(1)}, bf16[96,8192]{1,0:T(8,128)(2,1)}, u32[]{:S(2)}) copy-start(bf16[96,8192]{1,0:T(8,128)(2,1)} %param.6) | copy-start | bytes 4718596
  7.2 80.0 %all-gather.8.cloned.1.call-start = ((), (), s32[]{:S(2)}) async-start(), calls=%async_computation.3 | async-start | bytes 8912896 | tf_op jit(solution)/shard_map/all_gather | solution.py:58
  7.9 154.4 %all-gather.14.cloned.1.call-start = ((), (), s32[]{:S(2)}) async-start(), calls=%async_computation.6 | async-start | bytes 8912896 | tf_op jit(solution)/shard_map/all_gather | solution.py:59
  8.7 271.0 %all-gather.10.cloned.1.call-start = ((), (), s32[]{:S(2)}) async-start(), calls=%async_computation.4 | async-start | bytes 1671168 | tf_op jit(solution)/shard_map/all_gather | solution.py:93
  10.8 151.4 %copy-start.3 = (f32[8192]{0:T(1024)S(1)}, f32[8192]{0:T(1024)}, u32[]{:S(2)}) copy-start(f32[8192]{0:T(1024)} %param.7) | copy-start | bytes 98308
  93.2 188.2 %all-gather.16.cloned.1.call-start = ((), (), s32[]{:S(2)}) async-start(), calls=%async_computation.7 | async-start | bytes 1671168 | tf_op jit(solution)/shard_map/all_gather | solution.py:94
  167.8 244.8 %all-gather.12.cloned.1.call-start = ((), (), s32[]{:S(2)}) async-start(), calls=%async_computation.5 | async-start | bytes 35651584 | tf_op jit(solution)/shard_map/all_gather | solution.py:57
  168.4 12.2 %all-to-all-start.1 = ((bf16[2,256,512]{2,1,0:T(8,128)(2,1)}), bf16[2,256,512]{2,1,0:T(8,128)(2,1)S(1)}, u32[]{:S(2)}, u32[]{:S(2)}) async-start(bf16[2,256,512]{2,1,0:T(8,128)(2,1)} %bitcast.13), calls=%async_computation.1 | async-start | bytes 1048576 | tf_op jit(solution)/shard_map/all_to_all | solution.py:53
  176.5 78.5 %copy-start.10 = (u32[32]{0:T(128)S(1)}, u32[32]{0:T(128)}, u32[]{:S(2)}) copy-start(u32[32]{0:T(128)} %constant.46) | copy-start | bytes 388
  176.5 79.8 %copy-start.9 = (s32[96]{0:T(128)S(1)}, s32[96]{0:T(128)}, u32[]{:S(2)}) copy-start(s32[96]{0:T(128)} %param.11) | copy-start | bytes 1156
  180.6 69.4 %all-to-all-start.2 = ((bf16[2,256,512]{2,1,0:T(8,128)(2,1)}), bf16[2,256,512]{2,1,0:T(8,128)(2,1)S(1)}, u32[]{:S(2)}, u32[]{:S(2)}) async-start(bf16[2,256,512]{2,1,0:T(8,128)(2,1)} %bitcast.18), calls=%async_computation.2 | async-start | bytes 1048576 | tf_op jit(solution)/shard_map/all_to_all | solution.py:54
  250.0 25.7 %all-to-all-start = ((bf16[2,256,2048]{2,1,0:T(8,128)(2,1)}), bf16[2,256,2048]{2,1,0:T(8,128)(2,1)}, u32[]{:S(2)}, u32[]{:S(2)}) async-start(bf16[2,256,2048]{2,1,0:T(8,128)(2,1)} %bitcast.73), calls=%async_computation | async-start | bytes 4194304 | tf_op jit(solution)/shard_map/all_to_all | solution.py:52
  428.8 2.8 copy-start.4
  431.6 72.6 %copy-start.1 = (bf16[2,256,512]{1,2,0:T(8,128)(2,1)S(1)}, bf16[2,256,512]{1,2,0:T(8,128)(2,1)}, u32[]{:S(2)}) copy-start(bf16[2,256,512]{1,2,0:T(8,128)(2,1)} %copy.43) | copy-start | bytes 1572868
  431.6 72.6 %copy-start.2 = (bf16[2,256,512]{1,2,0:T(8,128)(2,1)S(1)}, bf16[2,256,512]{1,2,0:T(8,128)(2,1)}, u32[]{:S(2)}) copy-start(bf16[2,256,512]{1,2,0:T(8,128)(2,1)} %copy.44) | copy-start | bytes 1572868
  495.4 11.7 %copy-start.7 = (f32[512]{0:T(512)}, f32[512]{0:T(512)S(1)}, u32[]{:S(2)}) copy-start(f32[512]{0:T(512)S(1)} %maximum_multiply_fusion.2) | copy-start | bytes 6148
  499.8 7.3 %copy-start.8 = (f32[512]{0:T(512)}, f32[512]{0:T(512)S(1)}, u32[]{:S(2)}) copy-start(f32[512]{0:T(512)S(1)} %maximum_multiply_fusion.1) | copy-start | bytes 6148
  507.1 7.9 %copy-start.6 = (f32[2048]{0:T(1024)}, f32[2048]{0:T(1024)S(1)}, u32[]{:S(2)}) copy-start(f32[2048]{0:T(1024)S(1)} %maximum_multiply_fusion) | copy-start | bytes 24580
  515.0 5.7 %copy-start.5 = (bf16[96,4,4,128]{3,0,2,1:T(8,128)(2,1)S(1)}, bf16[96,4,4,128]{3,0,2,1:T(8,128)(2,1)}, u32[]{:S(2)}) copy-start(bf16[96,4,4,128]{3,0,2,1:T(8,128)(2,1)} %get-tuple-element.37) | copy-start | bytes 1179652
Sparse Core Ops, SparseCore 0:
  10.2 77.0 all-gather.7
  89.4 72.8 all-gather.13
  165.1 38.0 all-gather.9
  205.4 38.4 all-gather.15
  245.3 167.2 all-gather.11
where the time goes:
time: 529 us; the launch traced here: 528 us
  waiting for transfers between devices  283 us (53%)
  blocking collectives  148 us (28%)
  matrix products  29 us (5%)
  local copies, waits for them, and re-layouts  22.7 us (4%)
  other arithmetic  19.3 us (4%)
  between operations  14.7 us (3%)
  starting transfers between devices  12.1 us (2%)
    all_gather x1, waiting for transfers between devices, on_device(): lax.all_gather(w_query, 'tok', axis=0, tiled=True)  128 us
    all_gather x1, waiting for transfers between devices, on_device(): lax.all_gather(w_key, 'tok', axis=0, tiled=True)  76.4 us
    all_gather x1, waiting for transfers between devices, on_device(): lax.all_gather(w_value, 'tok', axis=0, tiled=True)  69 us
    pmax x1, blocking collectives, on_device(): lax.pmax(jnp.max(jnp.abs(attended), axis=0).astype(jnp.float32), 'tok')  60.6 us
    pmax x1, blocking collectives, on_device(): lax.pmax(jnp.max(jnp.abs(normed), axis=0).astype(jnp.float32).astype(jnp....  57.9 us
    dot_general x3, matrix products, on_device(): jnp.dot(normed, piece, preferred_element_type=jnp.float32)  23.9 us
    all_gather x3, blocking collectives, on_device(): every_scale = lax.all_gather(scales, 'tp', axis=0, tiled=True)  13.1 us
  transfers between devices with their start and end apart: 8, of which 5 were waited for; matrix products, arithmetic and copies ran while one was open for 7% of the time, Pallas kernels for 0%

commit v1 on v0

--- a/solution.py
+++ b/solution.py
@@ -29,6 +29,21 @@
     return jnp.sqrt(jnp.maximum(input_peak, 1e-05)) / jnp.sqrt(jnp.maximum(weight_peak, 1e-05))
 
 
+def head_to_rows(matrix, tp_index, tp_count):
+    sub_rows = matrix.shape[0] // tp_count
+    columns = matrix.shape[1]
+    whole = jnp.zeros((sub_rows, columns * tp_count), matrix.dtype)
+    for shift in range(tp_count):
+        target = lax.rem(tp_index + shift, tp_count)
+        source = lax.rem(tp_index - shift + tp_count, tp_count)
+        block = lax.dynamic_slice_in_dim(matrix, target * sub_rows, sub_rows)
+        if shift > 0:
+            pairs = [(i, (i + shift) % tp_count) for i in range(tp_count)]
+            block = lax.ppermute(block, "tp", pairs)
+        whole = lax.dynamic_update_slice_in_dim(whole, block, source * columns, axis=1)
+    return whole
+
+
 def on_device(hidden, norm_gain, w_query, w_key, w_value, doc_ids):
     tok_dev = hidden.shape[0]
     row_count = w_query.shape[0]
@@ -45,27 +60,23 @@
         * lax.rsqrt(jnp.mean(states * states, axis=1, keepdims=True) + 1e-05)
         * norm_gain[None, :]
     ).astype(jnp.bfloat16)
-    input_peak = lax.pmax(
-        jnp.max(jnp.abs(normed), axis=0).astype(jnp.float32).astype(jnp.bfloat16), "tok"
-    ).astype(jnp.float32)
-    relaid = (
-        lax.all_to_all(w_query, "tp", split_axis=0, concat_axis=1, tiled=True),
-        lax.all_to_all(w_key, "tp", split_axis=0, concat_axis=1, tiled=True),
-        lax.all_to_all(w_value, "tp", split_axis=0, concat_axis=1, tiled=True),
+    token_side = lax.all_to_all(normed, "tok", split_axis=1, concat_axis=0, tiled=True)
+    input_rows = jnp.max(jnp.abs(token_side), axis=0).astype(jnp.float32)
+    relaid = tuple(head_to_rows(matrix, tp_index, tp_count) for matrix in matrices)
+    partial = jnp.dot(
+        token_side, jnp.concatenate(matrices, axis=1), preferred_element_type=jnp.float32
     )
-    pieces = (
-        lax.all_gather(w_query, "tok", axis=0, tiled=True),
-        lax.all_gather(w_key, "tok", axis=0, tiled=True),
-        lax.all_gather(w_value, "tok", axis=0, tiled=True),
-    )
-    projected = tuple(
-        (jnp.dot(normed, piece, preferred_element_type=jnp.float32) for piece in pieces)
+    summed = lax.psum_scatter(partial, "tok", scatter_dimension=0, tiled=True)
+    query_columns, key_columns = w_query.shape[1], w_key.shape[1]
+    projected = (
+        summed[:, :query_columns],
+        summed[:, query_columns : query_columns + key_columns],
+        summed[:, query_columns + key_columns :],
     )
     local_peak = jnp.max(
         jnp.stack([jnp.max(jnp.abs(matrix), axis=1) for matrix in matrices]), axis=0
     ).astype(jnp.float32)
     row_peak = lax.pmax(local_peak, "tp")
-    input_rows = lax.dynamic_slice_in_dim(input_peak, tok_index * row_count, row_count)
     smoothing_rows = smooth_from(input_rows, row_peak)
     column_local = tuple(
         (

time: 529 us -> 444 us (0.84)
  waiting for transfers between devices: 283 us -> 218 us
  matrix products: 29 us -> 17.2 us
  blocking collectives: 148 us -> 138 us
  starting transfers between devices: 12.1 us -> 3.63 us
  other arithmetic: 19.3 us -> 24.6 us
    all_gather x3 -> x0, waiting for transfers between devices: 273 us -> none  [the longest x1 128 us: on_device(): lax.all_gather(w_query, 'tok', axis=0, tiled=True)]
    reduce_scatter x0 -> x1, waiting for transfers between devices: none -> 194 us  [on_device(): summed = lax.psum_scatter(partial, 'tok', scatter_dimension=0, tiled=True)]
    pmax x1 -> x0, blocking collectives: 57.9 us -> none  [on_device(): lax.pmax(jnp.max(jnp.abs(normed), axis=0).astype(jnp.float32).astype(jnp....]
    all_to_all x0 -> x1, blocking collectives: none -> 43.3 us  [on_device(): lax.all_to_all(normed, 'tok', split_axis=1, concat_axis=0, tiled=True)]
    all_gather x1, waiting for transfers between devices: 0.02 us -> 24.2 us  [on_device(): value_block = lax.all_gather(value, 'tok', axis=0, tiled=True)]
    dot_general x3 -> x1, matrix products: 23.9 us -> 9.24 us  [on_device(): jnp.dot(token_side, jnp.concatenate(matrices, axis=1), preferred_element_...]
    all_to_all x3 -> x0, starting transfers between devices: 11.9 us -> none  [the longest x1 4.93 us: on_device(): lax.all_to_all(w_query, 'tp', split_axis=0, concat_axis=1, tiled=True)]
    all_to_all x3 -> x0, waiting for transfers between devices: 8.14 us -> none  [the longest x1 4.53 us: on_device(): lax.all_to_all(w_query, 'tp', split_axis=0, concat_axis=1, tiled=True)]
  transfers between devices with their start and end apart: 8 -> 6, of which waited for: 5 -> 2; matrix products, arithmetic and copies ran while one was open for 7% -> 7% of each run, Pallas kernels for 0% -> 0%
where the time goes in v1:
time: 444 us; the launch traced here: 443 us
  waiting for transfers between devices  218 us (49%)
  blocking collectives  138 us (31%)
  local copies, waits for them, and re-layouts  27 us (6%)
  other arithmetic  24.6 us (6%)
  matrix products  17.2 us (4%)
  between operations  14.7 us (3%)
    reduce_scatter x1, waiting for transfers between devices, on_device(): summed = lax.psum_scatter(partial, 'tok', scatter_dimension=0, tiled=True)  194 us
    pmax x1, blocking collectives, on_device(): lax.pmax(jnp.max(jnp.abs(attended), axis=0).astype(jnp.float32), 'tok')  59.4 us
    all_to_all x1, blocking collectives, on_device(): lax.all_to_all(normed, 'tok', split_axis=1, concat_axis=0, tiled=True)  43.3 us
    all_gather x1, waiting for transfers between devices, on_device(): value_block = lax.all_gather(value, 'tok', axis=0, tiled=True)  24.2 us
    all_gather x3, blocking collectives, on_device(): every_scale = lax.all_gather(scales, 'tp', axis=0, tiled=True)  13.1 us
    pmax x1, blocking collectives, on_device(): row_peak = lax.pmax(local_peak, 'tp')  11.3 us
    unnamed x1, blocking collectives  10.8 us
    dot_general x1, matrix products, on_device(): jnp.dot(token_side, jnp.concatenate(matrices, axis=1), preferred_element_...  9.24 us
  transfers between devices with their start and end apart: 6, of which 2 were waited for; matrix products, arithmetic and copies ran while one was open for 7% of the time, Pallas kernels for 0%

profile of v1, /device:TPU:0, one launch (start us, length us, event | category | flops | bytes accessed | tf_op | source)
XLA Modules:
  0.0 442.9 jit_solution(13857068211997247535)
XLA Ops:
  7.2 1.8 fusion.6
  9.1 1.9 fusion.8
  11.1 43.3 %all_to_all.19 = bf16[96,16,512]{2,0,1:T(8,128)(2,1)S(1)} all-to-all(bf16[96,16,512]{2,0,1:T(8,128)(2,1)S(1)} %bitcast.63), channel_id=1, replica_groups=mesh['tok'=16,'tp'=2] {'tok'}, dimensions={1} | all-to-all | bytes 3145728 | tf_op jit(solution)/shard_map/all_to_all | solution.py:63
  55.5 9.2 %fusion.9 = f32[1536,3072]{1,0:T(8,128)} fusion(bf16[1536,512]{1,0:T(8,128)(2,1)S(1)} %bitcast.62, bf16[512,512]{1,0:T(8,128)(2,1)S(1)} %copy-done.3, bf16[512,512]{1,0:T(8,128)(2,1)S(1)} %copy-done.4, bf16[512,2048]{1,0:T(8,128)(2,1)S(1)} %copy-done.1), kind=kOutput, calls=%fused_computation.14 | convolution fusion | flops 4841275392 | bytes 23592960 | tf_op jit(solution)/shard_map/dot_general | solution.py:66
  65.8 193.7 %reduce-scatter.2.cloned.1.call-done = f32[96,3072]{1,0:T(8,128)} async-done(((f32[1536,3072]{1,0:T(8,128)}), f32[96,3072]{1,0:T(8,128)}) %reduce-scatter.2.cloned.1.call-update) | async-done | bytes 1179664 | tf_op jit(solution)/shard_map/reduce_scatter | solution.py:69
  273.9 10.8 %all-reduce = s32[1536]{0:T(1024)} all-reduce(s32[1536]{0:T(1024)S(1)} %dynamic-update-slice), channel_id=1, replica_groups=mesh['tok'=16,'tp'=2] {'tok'}, use_global_device_ids=true, to_apply=%add | all-reduce | flops 1536 | bytes 12288
  289.5 11.3 %pmax.36 = f32[512]{0:T(512)} all-reduce(f32[512]{0:T(512)} %maximum_convert_fusion), channel_id=1, replica_groups=mesh['tok'=16,'tp'=2] {'tp'}, use_global_device_ids=true, to_apply=%region_10.0 | all-reduce | flops 512 | bytes 4096 | tf_op jit(solution)/shard_map/pmax | solution.py:79
  300.8 1.7 constant_dynamic-update-slice_fusion
  302.5 1.7 constant_dynamic-update-slice_fusion.1
  304.2 2.3 constant_dynamic-update-slice_fusion.2
  308.1 1.7 fusion.16
  312.9 1.7 copy.32
  314.6 2.0 fusion
  316.6 3.6 copy-done
  320.2 2.8 fusion.1
  323.0 24.2 %all-gather.7.cloned.1.call-done = bf16[1536,512]{1,0:T(8,128)(2,1)} async-done(((bf16[96,512]{1,0:T(8,128)(2,1)}), bf16[1536,512]{1,0:T(8,128)(2,1)}) %all-gather.7.cloned.1.call-update) | async-done | bytes 1572880 | tf_op jit(solution)/shard_map/all_gather | solution.py:105
  347.2 2.4 reshape.131
  349.6 6.0 %abs_reduce_fusion.6 = (bf16[4,4,128]{2,1,0:T(4,128)(2,1)S(1)}, bf16[96,4,4,128]{3,0,2,1:T(8,128)(2,1)S(1)}) fusion(f32[96,4,4]{0,2,1:T(4,128)S(1)} %bitcast.72, bf16[1536,4,128,1]{2,1,0,3:T(4,128)(2,1)S(1)} %bitcast.65, f32[4,1536,96,4]{1,2,3,0:T(8,128)} %copy-done, f32[4,4,96]{2,1,0:T(4,128)S(1)} %broadcast_maximum_fusion, pred[96,1536]{1,0:T(8,128)(4,1)S(1)} %fusion.32), kind=kOutput, calls=%fused_computation.44 | convolution fusion | flops 616560640 | bytes 11567104 | tf_op jit(solution)/shard_map/kgts,skd->kgtd/dot_general | solution.py:125
  355.6 59.4 %all-reduce.1 = (f32[2048]{0:T(1024)}, f32[2048]{0:T(1024)S(1)}, f32[512]{0:T(512)S(1)}, f32[512]{0:T(512)S(1)}) all-reduce(bf16[2048]{0:T(1024)(128)(2,1)S(1)} %bitcast.75, f32[2048]{0:T(1024)S(1)} %abs_reduce_fusion, f32[512]{0:T(512)S(1)} %get-tuple-element.10, f32[512]{0:T(512)S(1)} %get-tuple-element.9), channel_id=1, replica_groups=mesh['tok'=16,'tp'=2] {'tok'}, use_global_device_ids=true, to_apply=%region_5.0 | all-reduce | flops 5120 | bytes 36864 | tf_op jit(solution)/shard_map/pmax | solution.py:138
  415.0 4.4 all-gather
  419.3 4.4 all-gather.1
  423.7 4.4 all_gather.21
  429.3 4.3 multiply_divide_fusion
  433.6 2.8 multiply_divide_fusion.1
  (81 shorter events, 26.7 us)
Async XLA Ops:
  7.2 252.2 %reduce-scatter.2.cloned.1.call-start = ((), (), s32[]{:S(2)}) async-start(), calls=%async_computation.2 | async-start | bytes 20054016 | tf_op jit(solution)/shard_map/reduce_scatter | solution.py:69
  10.9 44.6 %copy-start.1 = (bf16[512,2048]{1,0:T(8,128)(2,1)S(1)}, bf16[512,2048]{1,0:T(8,128)(2,1)}, u32[]{:S(2)}) copy-start(bf16[512,2048]{1,0:T(8,128)(2,1)} %param.8) | copy-start | bytes 6291460
  10.9 44.6 %copy-start.3 = (bf16[512,512]{1,0:T(8,128)(2,1)S(1)}, bf16[512,512]{1,0:T(8,128)(2,1)}, u32[]{:S(2)}) copy-start(bf16[512,512]{1,0:T(8,128)(2,1)} %param.10) | copy-start | bytes 1572868
  11.0 44.6 %copy-start.4 = (bf16[512,512]{1,0:T(8,128)(2,1)S(1)}, bf16[512,512]{1,0:T(8,128)(2,1)}, u32[]{:S(2)}) copy-start(bf16[512,512]{1,0:T(8,128)(2,1)} %param.9) | copy-start | bytes 1572868
  54.4 1.1 copy-start.2
  64.8 248.1 %all-gather.5.cloned.1.call-start = ((), (), s32[]{:S(2)}) async-start(), calls=%async_computation.3 | async-start | bytes 1671168 | tf_op jit(solution)/shard_map/all_gather | solution.py:104
  262.3 85.0 %all-gather.7.cloned.1.call-start = ((), (), s32[]{:S(2)}) async-start(), calls=%async_computation.4 | async-start | bytes 1671168 | tf_op jit(solution)/shard_map/all_gather | solution.py:105
  264.1 36.7 %collective-permute-start.2 = (bf16[256,512]{1,0:T(8,128)(2,1)S(1)}, bf16[256,512]{1,0:T(8,128)(2,1)}, u32[]{:S(2)}, u32[]{:S(2)}) collective-permute-start(bf16[256,512]{1,0:T(8,128)(2,1)S(1)} %get-tuple-element.21), channel_id=1, source_target_pairs={{0,1},{1,0},{2,3},{3,2},{4,5},{5,4},{6,7},{7,6},{8,9},{9,8},{10,11... | collective-permute-start | bytes 786440 | tf_op jit(solution)/shard_map/ppermute | solution.py:42
  267.2 35.3 %collective-permute-start.1 = (bf16[256,512]{1,0:T(8,128)(2,1)}, bf16[256,512]{1,0:T(8,128)(2,1)}, u32[]{:S(2)}, u32[]{:S(2)}) collective-permute-start(bf16[256,512]{1,0:T(8,128)(2,1)} %get-tuple-element.23), channel_id=1, source_target_pairs={{0,1},{1,0},{2,3},{3,2},{4,5},{5,4},{6,7},{7,6},{8,9},{9,8},{10,11... | collective-permute-start | bytes 786440 | tf_op jit(solution)/shard_map/ppermute | solution.py:42
  267.8 4.6 %copy-start.13 = (u32[32]{0:T(128)S(1)}, u32[32]{0:T(128)}, u32[]{:S(2)}) copy-start(u32[32]{0:T(128)} %constant.69) | copy-start | bytes 388
  267.8 5.9 %copy-start.12 = (s32[96]{0:T(128)S(1)}, s32[96]{0:T(128)}, u32[]{:S(2)}) copy-start(s32[96]{0:T(128)} %param.11) | copy-start | bytes 1156
  270.9 33.3 %collective-permute-start = (bf16[256,2048]{1,0:T(8,128)(2,1)}, bf16[256,2048]{1,0:T(8,128)(2,1)}, u32[]{:S(2)}, u32[]{:S(2)}) collective-permute-start(bf16[256,2048]{1,0:T(8,128)(2,1)} %get-tuple-element.17), channel_id=1, source_target_pairs={{0,1},{1,0},{2,3},{3,2},{4,5},{5,4},{6,7},{7,6},{8,9},{9,8},{10,11... | collective-permute-start | bytes 3145736 | tf_op jit(solution)/shard_map/ppermute | solution.py:42
  300.8 9.0 %copy-start.11 = (f32[512]{0:T(512)S(1)}, f32[512]{0:T(512)}, u32[]{:S(2)}) copy-start(f32[512]{0:T(512)} %pmax.36) | copy-start | bytes 6148
  308.1 3.9 copy-start.5
  311.2 1.1 copy-start.6
  311.2 1.1 copy-start.7
  316.6 3.6 copy-start
  415.0 18.6 %copy-start.9 = (f32[512]{0:T(512)}, f32[512]{0:T(512)S(1)}, u32[]{:S(2)}) copy-start(f32[512]{0:T(512)S(1)} %maximum_multiply_fusion.2) | copy-start | bytes 6148
  419.3 14.3 %copy-start.10 = (f32[512]{0:T(512)}, f32[512]{0:T(512)S(1)}, u32[]{:S(2)}) copy-start(f32[512]{0:T(512)S(1)} %maximum_multiply_fusion.1) | copy-start | bytes 6148
  423.7 9.9 %copy-start.8 = (f32[2048]{0:T(1024)}, f32[2048]{0:T(1024)S(1)}, u32[]{:S(2)}) copy-start(f32[2048]{0:T(1024)S(1)} %maximum_multiply_fusion) | copy-start | bytes 24580
Sparse Core Ops, SparseCore 0:
  64.9 194.4 reduce-scatter.1
  262.4 38.6 all-gather.4
  308.3 38.9 all-gather.6

commit v2 on v0

--- a/solution.py
+++ b/solution.py
@@ -1,8 +1,11 @@
+import functools
 import math
 
 import jax
 import jax.numpy as jnp
 from jax import lax
+from jax.experimental import pallas as pl
+from jax.experimental.pallas import tpu as pltpu
 from jax.sharding import PartitionSpec as P
 
 HEAD = 128
@@ -27,6 +30,331 @@
 
 def smooth_from(input_peak, weight_peak):
     return jnp.sqrt(jnp.maximum(input_peak, 1e-05)) / jnp.sqrt(jnp.maximum(weight_peak, 1e-05))
+
+
+MESH = pl.DeviceIdType.MESH
+QUAD = 4
+
+
+def column_chunks(widths, most=512):
+    return [
+        (which, start, min(most, width - start))
+        for which, width in enumerate(widths)
+        for start in range(0, width, most)
+    ]
+
+
+def front_kernel(
+    chunks,
+    line,
+    tp_count,
+    normed_ref,
+    wq_ref,
+    wk_ref,
+    wv_ref,
+    sum_ref,
+    peak_ref,
+    rq_ref,
+    rk_ref,
+    rv_ref,
+    held_q,
+    held_k,
+    held_v,
+    tokens,
+    partial,
+    from_left,
+    from_right,
+    w_send,
+    w_recv,
+    t_send,
+    t_recv,
+    x_send,
+    x_recv,
+    x_local,
+    r_send,
+    r_recv,
+    l_send,
+    l_recv,
+):
+    me = lax.axis_index("tok")
+    tp = lax.axis_index("tp")
+    quad = lax.rem(me, QUAD)
+    place = me // QUAD
+    rows = wq_ref.shape[0]
+    tok_dev = normed_ref.shape[0]
+    sib = me + 1 - 2 * lax.rem(me, 2)
+    side = me + 2 - 4 * (quad // 2)
+    side_sib = side + 1 - 2 * lax.rem(me, 2)
+    own = (wq_ref, wk_ref, wv_ref)
+    held = (held_q, held_k, held_v)
+    relaid = (rq_ref, rk_ref, rv_ref)
+    sub = rows // tp_count
+
+    def remote(src, dst, send, recv, tok, tp_to=None):
+        return pltpu.make_async_remote_copy(
+            src_ref=src,
+            dst_ref=dst,
+            send_sem=send,
+            recv_sem=recv,
+            device_id=(tok, tp if tp_to is None else tp_to),
+            device_id_type=MESH,
+        )
+
+    barrier = pltpu.get_barrier_semaphore()
+    pl.semaphore_signal(barrier, inc=1, device_id=(sib, tp), device_id_type=MESH)
+    pl.semaphore_signal(barrier, inc=1, device_id=(side, tp), device_id_type=MESH)
+    for step in range(1, line):
+        other = lax.rem(place + step, line) * QUAD + quad
+        pl.semaphore_signal(barrier, inc=1, device_id=(other, tp), device_id_type=MESH)
+    for step in range(1, tp_count):
+        other = lax.rem(tp + step, tp_count)
+        pl.semaphore_signal(barrier, inc=1, device_id=(me, other), device_id_type=MESH)
+    pl.semaphore_wait(barrier, 2 + (line - 1) + (tp_count - 1))
+
+    def w_copy(kind, c):
+        which, start, width = chunks[c]
+        cols = pl.ds(start, width)
+        if kind == 2:
+            src = held[which].at[1, :, cols]
+        else:
+            src = own[which].at[:, cols]
+        return remote(
+            src,
+            held[which].at[kind, :, cols],
+            w_send.at[kind, c],
+            w_recv.at[kind, c],
+            side if kind == 1 else sib,
+        )
+
+    def t_copy(step):
+        to = lax.rem(place + step, line)
+        width = QUAD * rows
+        return remote(
+            normed_ref.at[:, pl.ds(pl.multiple_of(to * width, 128), width)],
+            tokens.at[pl.ds(pl.multiple_of(place * tok_dev, 16), tok_dev)],
+            t_send.at[step],
+            t_recv.at[step],
+            to * QUAD + quad,
+        )
+
+    def x_copy(which, step):
+        to = lax.rem(tp + step, tp_count)
+        width = own[which].shape[1]
+        src = own[which].at[pl.ds(pl.multiple_of(to * sub, 16), sub)]
+        dst = relaid[which].at[:, pl.ds(pl.multiple_of(tp * width, 128), width)]
+        if step == 0:
+            return pltpu.make_async_copy(src, dst, x_local.at[which])
+        return remote(src, dst, x_send.at[which, step], x_recv.at[which, step], me, to)
+
+    for step in range(1, line):
+        t_copy(step).start()
+    for c in range(len(chunks)):
+        w_copy(1, c).start()
+        w_copy(0, c).start()
+    for which in range(3):
+        for step in range(tp_count):
+            x_copy(which, step).start()
+
+    width = QUAD * rows
+    tokens[pl.ds(pl.multiple_of(place * tok_dev, 16), tok_dev)] = normed_ref[
+        :, pl.ds(pl.multiple_of(place * width, 128), width)
+    ]
+    for step in range(1, line):
+        t_copy(step).wait_recv()
+    peak_ref[...] = jnp.max(
+        jnp.abs(tokens[...].astype(jnp.float32)), axis=0, keepdims=True
+    )
+
+    def span(c):
+        which, start, size = chunks[c]
+        base = sum(own[i].shape[1] for i in range(which)) + start
+        return slice(base, base + size)
+
+    def block(d):
+        return pl.ds(pl.multiple_of(d * tok_dev, 8), tok_dev)
+
+    def right(c, d):
+        cols = span(c)
+        return remote(
+            partial.at[block(d), cols],
+            from_left.at[block(d), cols],
+            r_send.at[c, d],
+            r_recv.at[c, d],
+            me + QUAD,
+        )
+
+    def left(c, d):
+        cols = span(c)
+        return remote(
+            partial.at[block(d), cols],
+            from_right.at[block(d), cols],
+            l_send.at[c, d],
+            l_recv.at[c, d],
+            me - QUAD,
+        )
+
+    def add_left(c, d):
+        right(c, d).wait_recv()
+        cols = span(c)
+        partial[block(d), cols] = partial[block(d), cols] + from_left[block(d), cols]
+
+    def add_right(c, d):
+        left(c, d).wait_recv()
+        cols = span(c)
+        partial[block(d), cols] = partial[block(d), cols] + from_right[block(d), cols]
+
+    def first_sends(c):
+        @pl.when(place == 0)
+        def _():
+            def go(i, carry):
+                right(c, line - 1 - i).start()
+                return carry
+
+            lax.fori_loop(0, line - 1, go, 0)
+
+        @pl.when(place == line - 1)
+        def _():
+            def go(i, carry):
+                left(c, i).start()
+                return carry
+
+            lax.fori_loop(0, line - 1, go, 0)
+
+    def reduce(c):
+        def go(i, carry):
+            to_right = line - 1 - i
+
+            @pl.when((place > 0) & (to_right > place))
+            def _():
+                add_left(c, to_right)
+                right(c, to_right).start()
+
+            @pl.when((place < line - 1) & (i < place))
+            def _():
+                add_right(c, i)
+                left(c, i).start()
+
+            return carry
+
+        lax.fori_loop(0, line, go, 0)
+
+        @pl.when(place > 0)
+        def _():
+            add_left(c, place)
+
+        @pl.when(place < line - 1)
+        def _():
+            add_right(c, place)
+
+        sum_ref[:, span(c)] = partial[block(place), span(c)]
+
+    def columns_of(tok):
+        return pl.ds(pl.multiple_of(lax.rem(tok, QUAD) * rows, 128), rows)
+
+    for c in range(len(chunks)):
+        which, start, size = chunks[c]
+        cols = slice(start, start + size)
+        w_copy(1, c).wait_recv()
+        w_copy(2, c).start()
+        total = jnp.dot(
+            tokens[:, columns_of(me)],
+            own[which][:, cols],
+            preferred_element_type=jnp.float32,
+        )
+        total += jnp.dot(
+            tokens[:, columns_of(side)],
+            held[which][1, :, cols],
+            preferred_element_type=jnp.float32,
+        )
+        w_copy(0, c).wait_recv()
+        total += jnp.dot(
+            tokens[:, columns_of(sib)],
+            held[which][0, :, cols],
+            preferred_element_type=jnp.float32,
+        )
+        w_copy(2, c).wait_recv()
+        total += jnp.dot(
+            tokens[:, columns_of(side_sib)],
+            held[which][2, :, cols],
+            preferred_element_type=jnp.float32,
+        )
+        partial[:, span(c)] = total
+        first_sends(c)
+        if c > 0:
+            reduce(c - 1)
+    reduce(len(chunks) - 1)
+
+    for step in range(1, line):
+        t_copy(step).wait_send()
+    for c in range(len(chunks)):
+        for kind in range(3):
+            w_copy(kind, c).wait_send()
+
+        def sent(d, carry):
+            @pl.when(d > place)
+            def _():
+                right(c, d).wait_send()
+
+            @pl.when(d < place)
+            def _():
+                left(c, d).wait_send()
+
+            return carry
+
+        lax.fori_loop(0, line, sent, 0)
+    for which in range(3):
+        x_copy(which, 0).wait()
+        for step in range(1, tp_count):
+            x_copy(which, step).wait_send()
+            x_copy(which, step).wait_recv()
+
+
+def front(normed, matrices):
+    tok_count, tp_count = lax.axis_size("tok"), lax.axis_size("tp")
+    line = tok_count // QUAD
+    tok_dev = normed.shape[0]
+    rows = matrices[0].shape[0]
+    widths = [matrix.shape[1] for matrix in matrices]
+    chunks = column_chunks(widths)
+    total = sum(widths)
+    vmem = pl.BlockSpec(memory_space=pltpu.VMEM)
+    dma = pltpu.SemaphoreType.DMA
+    return pl.pallas_call(
+        functools.partial(front_kernel, chunks, line, tp_count),
+        out_shape=(
+            jax.ShapeDtypeStruct((tok_dev, total), jnp.float32),
+            jax.ShapeDtypeStruct((1, QUAD * rows), jnp.float32),
+        )
+        + tuple(
+            jax.ShapeDtypeStruct((rows // tp_count, width * tp_count), jnp.bfloat16)
+            for width in widths
+        ),
+        in_specs=[vmem] * 4,
+        out_specs=(vmem, vmem) + (pl.BlockSpec(memory_space=pl.ANY),) * 3,
+        scratch_shapes=[
+            pltpu.VMEM((3, rows, width), jnp.bfloat16) for width in widths
+        ]
+        + [
+            pltpu.VMEM((line * tok_dev, QUAD * rows), jnp.bfloat16),
+            pltpu.VMEM((line * tok_dev, total), jnp.float32),
+            pltpu.VMEM((line * tok_dev, total), jnp.float32),
+            pltpu.VMEM((line * tok_dev, total), jnp.float32),
+            dma((3, len(chunks))),
+            dma((3, len(chunks))),
+            dma((line,)),
+            dma((line,)),
+            dma((3, tp_count)),
+            dma((3, tp_count)),
+            dma((3,)),
+            dma((len(chunks), line)),
+            dma((len(chunks), line)),
+            dma((len(chunks), line)),
+            dma((len(chunks), line)),
+        ],
+        compiler_params=pltpu.CompilerParams(
+            collective_id=0, has_side_effects=True, vmem_limit_bytes=60 * 1024 * 1024
+        ),
+    )(normed, *matrices)
 
 
 def on_device(hidden, norm_gain, w_query, w_key, w_value, doc_ids):
@@ -45,36 +373,39 @@
         * lax.rsqrt(jnp.mean(states * states, axis=1, keepdims=True) + 1e-05)
         * norm_gain[None, :]
     ).astype(jnp.bfloat16)
-    input_peak = lax.pmax(
-        jnp.max(jnp.abs(normed), axis=0).astype(jnp.float32).astype(jnp.bfloat16), "tok"
-    ).astype(jnp.float32)
-    relaid = (
-        lax.all_to_all(w_query, "tp", split_axis=0, concat_axis=1, tiled=True),
-        lax.all_to_all(w_key, "tp", split_axis=0, concat_axis=1, tiled=True),
-        lax.all_to_all(w_value, "tp", split_axis=0, concat_axis=1, tiled=True),
-    )
-    pieces = (
-        lax.all_gather(w_query, "tok", axis=0, tiled=True),
-        lax.all_gather(w_key, "tok", axis=0, tiled=True),
-        lax.all_gather(w_value, "tok", axis=0, tiled=True),
-    )
-    projected = tuple(
-        (jnp.dot(normed, piece, preferred_element_type=jnp.float32) for piece in pieces)
-    )
-    local_peak = jnp.max(
-        jnp.stack([jnp.max(jnp.abs(matrix), axis=1) for matrix in matrices]), axis=0
-    ).astype(jnp.float32)
-    row_peak = lax.pmax(local_peak, "tp")
-    input_rows = lax.dynamic_slice_in_dim(input_peak, tok_index * row_count, row_count)
-    smoothing_rows = smooth_from(input_rows, row_peak)
-    column_local = tuple(
-        (
-            jnp.max(jnp.abs(smoothing_rows[:, None] * matrix.astype(jnp.float32)), axis=0)
-            for matrix in matrices
-        )
-    )
-    column_global = lax.pmax(column_local, "tok")
-    scales = tuple((jnp.maximum(column, 1e-05) / 127.0 for column in column_global))
+    summed, peaks, *relaid = front(normed, matrices)
+    query_columns, key_columns = w_query.shape[1], w_key.shape[1]
+    projected = (
+        summed[:, :query_columns],
+        summed[:, query_columns : query_columns + key_columns],
+        summed[:, query_columns + key_columns :],
+    )
+    tok_count = lax.axis_size("tok")
+    quads = [[i + j for j in range(QUAD)] for i in range(0, tok_count, QUAD)]
+    quad_peak = lax.pmax(peaks[0], "tok", axis_index_groups=quads)
+    sub_rows = row_count // tp_count
+    smooth_part = smooth_from(
+        lax.dynamic_slice_in_dim(
+            quad_peak, (tok_index % QUAD) * row_count + tp_index * sub_rows, sub_rows
+        ),
+        functools.reduce(
+            jnp.maximum, [jnp.max(jnp.abs(block), axis=1) for block in relaid]
+        ).astype(jnp.float32),
+    )
+    column_local = jnp.concatenate(
+        [
+            jnp.max(jnp.abs(smooth_part[:, None] * block.astype(jnp.float32)), axis=0)
+            for block in relaid
+        ]
+    )
+    every = jnp.maximum(lax.pmax(column_local, ("tok", "tp")), 1e-05) / 127.0
+    every_scale = jnp.split(
+        every, [relaid[0].shape[1], relaid[0].shape[1] + relaid[1].shape[1]]
+    )
+    scales = tuple(
+        lax.dynamic_slice_in_dim(scale, tp_index * matrix.shape[1], matrix.shape[1])
+        for scale, matrix in zip(every_scale, matrices)
+    )
     query_positions = tok_index * tok_dev + jnp.arange(tok_dev, dtype=jnp.int32)
     positions = query_positions.astype(jnp.float32)
     query = (
@@ -90,8 +421,8 @@
     value = projected[2].astype(jnp.bfloat16)
     score_scale = 1.0 / math.sqrt(HEAD)
     highest = jnp.full((kv_here, group_size, tok_dev), -1e30, jnp.float32)
-    key_block = lax.all_gather(key, "tok", axis=0, tiled=True)
-    value_block = lax.all_gather(value, "tok", axis=0, tiled=True)
+    both = lax.all_gather(jnp.concatenate([key, value], axis=1), "tok", axis=0, tiled=True)
+    key_block, value_block = both[:, :key_columns], both[:, key_columns:]
     doc_block = lax.all_gather(doc_ids, "tok", axis=0, tiled=True)
     length = key_block.shape[0]
     scores = (
@@ -125,13 +456,10 @@
         .astype(jnp.bfloat16)
     )
     out_scale = lax.pmax(jnp.max(jnp.abs(attended), axis=0).astype(jnp.float32), "tok")
-    sub_rows = row_count // tp_count
-    smooth_part = lax.dynamic_slice_in_dim(smoothing_rows, tp_index * sub_rows, sub_rows)
     gain_part = lax.dynamic_slice_in_dim(
         norm_gain, tok_index * row_count + tp_index * sub_rows, sub_rows
     )
     folded_gain = gain_part / smooth_part
-    every_scale = lax.all_gather(scales, "tp", axis=0, tiled=True)
     codes = tuple(
         (
             smooth_part[:, None] * block.astype(jnp.float32) / column_scale[None, :]

time: 529 us -> 305 us (0.58)
  waiting for transfers between devices: 283 us -> 0.02 us
  Pallas kernels: 0 us -> 156 us
  blocking collectives: 148 us -> 88.9 us
  matrix products: 29 us -> 9.25 us
  starting transfers between devices: 12.1 us -> 0.04 us
  local copies, waits for them, and re-layouts: 22.7 us -> 15.5 us
    all_gather x5 -> x1, waiting for transfers between devices: 273 us -> 0.01 us  [on_device(): lax.all_gather(jnp.concatenate([key, value], axis=1), 'tok', axis=0, tile...]
    pallas_call x0 -> x1, Pallas kernels: none -> 156 us  [front(): pl.pallas_call(functools.partial(front_kernel, chunks, line, tp_count), o...]
    pmax x1, blocking collectives: 60.6 us -> 30.6 us  [on_device(): lax.pmax(jnp.max(jnp.abs(attended), axis=0).astype(jnp.float32), 'tok')]
    dot_general x3 -> x0, matrix products: 23.9 us -> none  [on_device(): jnp.dot(normed, piece, preferred_element_type=jnp.float32)]
    pmax x2, blocking collectives: 65.8 us -> 46.7 us  [the longest x1 41 us: on_device(): every = jnp.maximum(lax.pmax(column_local, ('tok', 'tp')), 1e-05) / 127.0]
    all_gather x3 -> x0, blocking collectives: 13.1 us -> none  [on_device(): every_scale = lax.all_gather(scales, 'tp', axis=0, tiled=True)]
    all_to_all x3 -> x0, starting transfers between devices: 11.9 us -> none  [the longest x1 4.93 us: on_device(): lax.all_to_all(w_query, 'tp', split_axis=0, concat_axis=1, tiled=True)]
    all_to_all x3 -> x0, waiting for transfers between devices: 8.14 us -> none  [the longest x1 4.53 us: on_device(): lax.all_to_all(w_query, 'tp', split_axis=0, concat_axis=1, tiled=True)]
  transfers between devices with their start and end apart: 8 -> 1, of which waited for: 5 -> 0; matrix products, arithmetic and copies ran while one was open for 7% -> 4% of each run, Pallas kernels for 0% -> 0%
where the time goes in v2:
time: 305 us
  Pallas kernels  156 us (51%)
  blocking collectives  88.9 us (29%)
  other arithmetic  20 us (7%)
  local copies, waits for them, and re-layouts  15.5 us (5%)
  between operations  15 us (5%)
  matrix products  9.25 us (3%)
    pallas_call x1, Pallas kernels, front(): pl.pallas_call(functools.partial(front_kernel, chunks, line, tp_count), o...  156 us
    pmax x1, blocking collectives, on_device(): every = jnp.maximum(lax.pmax(column_local, ('tok', 'tp')), 1e-05) / 127.0  41 us
    pmax x1, blocking collectives, on_device(): lax.pmax(jnp.max(jnp.abs(attended), axis=0).astype(jnp.float32), 'tok')  30.6 us
    unnamed x1, blocking collectives  11.6 us
    dot_general x1, matrix products, on_device(): jnp.einsum('tkgd,skd->kgts', query, key_block.reshape(length, kv_here, HE...  6.76 us
  transfers between devices with their start and end apart: 1, of which 0 were waited for; matrix products, arithmetic and copies ran while one was open for 4% of the time, Pallas kernels for 0%

profile of v2, /device:TPU:0, one launch (start us, length us, event | category | flops | bytes accessed | tf_op | source)
XLA Modules:
  0.0 304.6 jit_solution(7930155382110548142)
XLA Ops:
  7.2 1.8 fusion.7
  9.1 3.0 fusion.9.normed_ref
  12.1 155.9 %shard_map.133 = (f32[96,3072]{1,0:T(8,128)}, f32[1,2048]{1,0:T(1,128)}, bf16[256,4096]{1,0:T(8,128)(2,1)}, bf16[256,1024]{1,0:T(8,128)(2,1)}, bf16[256,1024]{1,0:T(8,128)(2,1)}) custom-call(bf16[96,8192]{1,0:T(8,128)(2,1)} %fusion.9.normed_ref, bf16[512,2048]{1,0:T(8,128)(2,1)} %wq_ref.1, bf16[512,512]{1,0:T(8,128)(2,1)} %wk_ref.1, bf16[512,512]{1,0:T(8,128)(2,1)} %wv_ref.1), custom_call_target="tpu_custom_call" | custom-call | tf_op jit(solution)/shard_map/pallas_call | solution.py:322
  168.0 0.9 slice.54
  168.9 0.9 slice.28
  170.6 0.7 pad_maximum_fusion
  171.4 1.3 slice_bitcast_fusion
  173.3 0.8 copy.20
  174.1 0.8 copy.19
  175.0 5.7 %pmax.22 = f32[2048]{0:T(1024)S(1)} all-reduce(f32[2048]{0:T(1024)S(1)} %bitcast.49), channel_id=1, replica_groups={{0,2,4,6},{8,10,12,14},{16,18,20,22},{24,26,28,30},{1,3,5,7},{9,11,13,1..., use_global_device_ids=true, to_apply=%region_5.6 | all-reduce | flops 2048 | bytes 16384 | tf_op jit(solution)/shard_map/pmax | solution.py:385
  181.5 1.3 dynamic-slice_divide_fusion
  183.6 41.0 %pmax.23 = f32[6144]{0:T(1024)S(1)} all-reduce(f32[6144]{0:T(1024)S(1)} %pad_maximum_fusion.2), channel_id=1, replica_groups=mesh['tok'=16,'tp'=2] {'tok','tp'}, use_global_device_ids=true, to_apply=%region_12.13 | all-reduce | flops 6144 | bytes 49152 | tf_op jit(solution)/shard_map/pmax | solution.py:401
  224.6 0.7 dynamic_slice.18
  225.3 0.6 dynamic_slice.19
  228.0 11.6 %all-reduce = s32[1536]{0:T(1024)S(1)} all-reduce(s32[1536]{0:T(1024)S(1)} %dynamic-update-slice), channel_id=1, replica_groups=mesh['tok'=16,'tp'=2] {'tok'}, use_global_device_ids=true, to_apply=%add | all-reduce | flops 1536 | bytes 12288
  239.6 1.6 fusion.18
  241.5 2.7 fusion.6
  244.2 3.2 %fusion.39 = (bf16[1536,512]{1,0:T(8,128)(2,1)}, bf16[1536,512]{1,0:T(8,128)(2,1)S(1)}) fusion(bf16[1536,1024]{1,0:T(8,128)(2,1)} %all-gather.2.cloned.1.call-done), kind=kLoop, calls=%fused_computation.60 | loop fusion | bytes 6291456 | tf_op jit(solution)/shard_map/slice | solution.py:425
  247.4 2.4 reshape.122
  249.8 6.8 %fusion = (f32[4,4,96]{2,1,0:T(4,128)S(1)}, f32[4,1536,96,4]{1,2,3,0:T(8,128)}) fusion(pred[96,1536]{1,0:T(8,128)(4,1)S(1)} %fusion.30, bf16[96,4,4,64]{3,0,2,1:T(8,128)(2,1)} %bitcast.43, bf16[96,4,4,64]{3,0,2,1:T(8,128)(2,1)} %bitcast.44, bf16[1536,4,128,1]{2,1,0,3:T(4,128)(2,1)S(1)} %bitcast.42), kind=kOutput, calls=%fused_computation.2 | convolution fusion | flops 611842560 | bytes 11556864 | tf_op jit(solution)/shard_map/tkgd,skd->kgts/dot_general | solution.py:429
  256.9 6.1 %fusion.1 = f32[4,4,96]{2,1,0:T(4,128)S(1)} fusion(f32[4,1536,96,4]{1,2,3,0:T(8,128)} %get-tuple-element.36, f32[4,4,96]{2,1,0:T(4,128)S(1)} %broadcast_maximum_fusion, pred[96,1536]{1,0:T(8,128)(4,1)S(1)} %fusion.30), kind=kLoop, calls=%fused_computation.3 | loop fusion | flops 11794944 | bytes 9596928 | tf_op jit(solution)/shard_map/reduce_sum | solution.py:444
  263.4 2.5 abs_reduce_fusion.6
  266.1 1.0 convert_element_type.58
  267.1 30.6 %pmax.21 = f32[2048]{0:T(1024)} all-reduce(bf16[2048]{0:T(1024)(128)(2,1)S(1)} %bitcast.50), channel_id=1, replica_groups=mesh['tok'=16,'tp'=2] {'tok'}, use_global_device_ids=true, to_apply=%region_4.5 | all-reduce | flops 2048 | bytes 12288 | tf_op jit(solution)/shard_map/pmax | solution.py:458
  (44 shorter events, 5.5 us)
Async XLA Ops:
  7.2 237.0 %all-gather.2.cloned.1.call-start = ((), (), s32[]{:S(2)}) async-start(), calls=%async_computation | async-start | bytes 3342336 | tf_op jit(solution)/shard_map/all_gather | solution.py:424
  170.4 4.5 %copy-start.4 = (f32[1,2048]{1,0:T(1,128)S(1)}, f32[1,2048]{1,0:T(1,128)}, u32[]{:S(2)}) copy-start(f32[1,2048]{1,0:T(1,128)} %get-tuple-element.15) | copy-start | bytes 24580
  170.4 10.3 %copy-start.2 = (bf16[256,1024]{1,0:T(8,128)(2,1)S(1)}, bf16[256,1024]{1,0:T(8,128)(2,1)}, u32[]{:S(2)}) copy-start(bf16[256,1024]{1,0:T(8,128)(2,1)} %get-tuple-element.17) | copy-start | bytes 1572868
  170.5 10.3 %copy-start.3 = (bf16[256,1024]{1,0:T(8,128)(2,1)S(1)}, bf16[256,1024]{1,0:T(8,128)(2,1)}, u32[]{:S(2)}) copy-start(bf16[256,1024]{1,0:T(8,128)(2,1)} %get-tuple-element.18) | copy-start | bytes 1572868
  171.3 9.7 %copy-start.1 = (bf16[256,4096]{1,0:T(8,128)(2,1)S(1)}, bf16[256,4096]{1,0:T(8,128)(2,1)}, u32[]{:S(2)}) copy-start(bf16[256,4096]{1,0:T(8,128)(2,1)} %get-tuple-element.16) | copy-start | bytes 6291460
  173.3 52.7 %copy-start.6 = (u32[32]{0:T(128)S(1)}, u32[32]{0:T(128)}, u32[]{:S(2)}) copy-start(u32[32]{0:T(128)} %constant.61) | copy-start | bytes 388
  173.3 54.5 %copy-start.5 = (s32[96]{0:T(128)S(1)}, s32[96]{0:T(128)}, u32[]{:S(2)}) copy-start(s32[96]{0:T(128)} %param.11) | copy-start | bytes 1156
  256.9 6.4 %copy-start = (f32[4,1536,96,4]{1,2,3,0:T(8,128)S(1)}, f32[4,1536,96,4]{1,2,3,0:T(8,128)}, u32[]{:S(2)}) copy-start(f32[4,1536,96,4]{1,2,3,0:T(8,128)} %get-tuple-element.36) | copy-start | bytes 28311556
Sparse Core Ops, SparseCore 0:
  171.5 45.0 all-gather.1

commit v3 on v2

--- a/solution.py
+++ b/solution.py
@@ -44,19 +44,36 @@
     ]
 
 
+def meet_all(barrier, me, tp, tok_count, tp_count):
+    def greet(step, carry):
+        other = lax.rem(me + step, tok_count)
+        pl.semaphore_signal(barrier, inc=1, device_id=(other, tp), device_id_type=MESH)
+        return carry
+
+    lax.fori_loop(1, tok_count, greet, 0)
+    for step in range(1, tp_count):
+        other = lax.rem(tp + step, tp_count)
+        pl.semaphore_signal(barrier, inc=1, device_id=(me, other), device_id_type=MESH)
+    pl.semaphore_wait(barrier, tok_count - 1 + tp_count - 1)
+
+
 def front_kernel(
     chunks,
     line,
     tp_count,
     normed_ref,
+    doc_ref,
     wq_ref,
     wk_ref,
     wv_ref,
     sum_ref,
     peak_ref,
+    docs_ref,
     rq_ref,
     rk_ref,
     rv_ref,
+    mine,
+    theirs,
     held_q,
     held_k,
     held_v,
@@ -75,6 +92,10 @@
     r_recv,
     l_send,
     l_recv,
+    p_send,
+    p_recv,
+    d_send,
+    d_recv,
 ):
     me = lax.axis_index("tok")
     tp = lax.axis_index("tp")
@@ -101,15 +122,7 @@
         )
 
     barrier = pltpu.get_barrier_semaphore()
-    pl.semaphore_signal(barrier, inc=1, device_id=(sib, tp), device_id_type=MESH)
-    pl.semaphore_signal(barrier, inc=1, device_id=(side, tp), device_id_type=MESH)
-    for step in range(1, line):
-        other = lax.rem(place + step, line) * QUAD + quad
-        pl.semaphore_signal(barrier, inc=1, device_id=(other, tp), device_id_type=MESH)
-    for step in range(1, tp_count):
-        other = lax.rem(tp + step, tp_count)
-        pl.semaphore_signal(barrier, inc=1, device_id=(me, other), device_id_type=MESH)
-    pl.semaphore_wait(barrier, 2 + (line - 1) + (tp_count - 1))
+    meet_all(barrier, me, tp, line * QUAD, tp_count)
 
     def w_copy(kind, c):
         which, start, width = chunks[c]
@@ -146,6 +159,32 @@
             return pltpu.make_async_copy(src, dst, x_local.at[which])
         return remote(src, dst, x_send.at[which, step], x_recv.at[which, step], me, to)
 
+    def d_copy(step):
+        return remote(
+            doc_ref,
+            docs_ref.at[me],
+            d_send.at[step],
+            d_recv.at[step],
+            lax.rem(me + step, line * QUAD),
+        )
+
+    def p_copy(kind):
+        return remote(
+            mine,
+            theirs.at[kind],
+            p_send.at[kind],
+            p_recv.at[kind],
+            (sib, side, side_sib)[kind],
+        )
+
+    def d_start(step, carry):
+        d_copy(step).start()
+        return carry
+
+    def d_wait(step, carry):
+        d_copy(step).wait()
+        return carry
+
     for step in range(1, line):
         t_copy(step).start()
     for c in range(len(chunks)):
@@ -161,9 +200,11 @@
     ]
     for step in range(1, line):
         t_copy(step).wait_recv()
-    peak_ref[...] = jnp.max(
+    mine[...] = jnp.max(
         jnp.abs(tokens[...].astype(jnp.float32)), axis=0, keepdims=True
     )
+    docs_ref[me] = doc_ref[...]
+    lax.fori_loop(1, line * QUAD, d_start, 0)
 
     def span(c):
         which, start, size = chunks[c]
@@ -280,10 +321,19 @@
         )
         partial[:, span(c)] = total
         first_sends(c)
+        if c == 0:
+            for kind in range(3):
+                p_copy(kind).start()
         if c > 0:
             reduce(c - 1)
     reduce(len(chunks) - 1)
 
+    for kind in range(3):
+        p_copy(kind).wait()
+    peak_ref[...] = jnp.maximum(
+        jnp.maximum(mine[...], theirs[0]), jnp.maximum(theirs[1], theirs[2])
+    )
+    lax.fori_loop(1, line * QUAD, d_wait, 0)
     for step in range(1, line):
         t_copy(step).wait_send()
     for c in range(len(chunks)):
@@ -309,7 +359,7 @@
             x_copy(which, step).wait_recv()
 
 
-def front(normed, matrices):
+def front(normed, doc_row, matrices):
     tok_count, tp_count = lax.axis_size("tok"), lax.axis_size("tp")
     line = tok_count // QUAD
     tok_dev = normed.shape[0]
@@ -324,14 +374,19 @@
         out_shape=(
             jax.ShapeDtypeStruct((tok_dev, total), jnp.float32),
             jax.ShapeDtypeStruct((1, QUAD * rows), jnp.float32),
+            jax.ShapeDtypeStruct((tok_count,) + doc_row.shape, jnp.int32),
         )
         + tuple(
             jax.ShapeDtypeStruct((rows // tp_count, width * tp_count), jnp.bfloat16)
             for width in widths
         ),
-        in_specs=[vmem] * 4,
-        out_specs=(vmem, vmem) + (pl.BlockSpec(memory_space=pl.ANY),) * 3,
+        in_specs=[vmem] * 5,
+        out_specs=(vmem, vmem, vmem) + (pl.BlockSpec(memory_space=pl.ANY),) * 3,
         scratch_shapes=[
+            pltpu.VMEM((1, QUAD * rows), jnp.float32),
+            pltpu.VMEM((3, 1, QUAD * rows), jnp.float32),
+        ]
+        + [
             pltpu.VMEM((3, rows, width), jnp.bfloat16) for width in widths
         ]
         + [
@@ -350,11 +405,233 @@
             dma((len(chunks), line)),
             dma((len(chunks), line)),
             dma((len(chunks), line)),
+            dma((3,)),
+            dma((3,)),
+            dma((tok_count,)),
+            dma((tok_count,)),
         ],
         compiler_params=pltpu.CompilerParams(
             collective_id=0, has_side_effects=True, vmem_limit_bytes=60 * 1024 * 1024
         ),
-    )(normed, *matrices)
+    )(normed, doc_row, *matrices)
+
+
+def back_kernel(
+    line,
+    tp_count,
+    kv_here,
+    query_ref,
+    kv_ref,
+    doc_mine_ref,
+    doc_all_ref,
+    column_ref,
+    out_ref,
+    out_peak_ref,
+    scale_ref,
+    cache,
+    column_tp,
+    column_mid,
+    column_all,
+    out_mine,
+    out_all,
+    z_send,
+    z_recv,
+    y_send,
+    y_recv,
+    s_send,
+    s_recv,
+    c_send,
+    c_recv,
+    a_send,
+    a_recv,
+    o_send,
+    o_recv,
+):
+    me = lax.axis_index("tok")
+    tp = lax.axis_index("tp")
+    tok_count = line * QUAD
+    quad = lax.rem(me, QUAD)
+    place = me // QUAD
+    tok_dev = query_ref.shape[0]
+    keys = cache.shape[0]
+    sib = me + 1 - 2 * lax.rem(me, 2)
+    side = me + 2 - 4 * (quad // 2)
+
+    def remote(src, dst, send, recv, tok, tp_to=None):
+        return pltpu.make_async_remote_copy(
+            src_ref=src,
+            dst_ref=dst,
+            send_sem=send,
+            recv_sem=recv,
+            device_id=(tok, tp if tp_to is None else tp_to),
+            device_id_type=MESH,
+        )
+
+    def rows_of(tok):
+        return pl.ds(pl.multiple_of(tok * tok_dev, 16), tok_dev)
+
+    def z_copy(step):
+        to = lax.rem(place + step, line) * QUAD + quad
+        return remote(
+            kv_ref, cache.at[rows_of(me)], z_send.at[step], z_recv.at[step], to
+        )
+
+    def line_source(step):
+        return lax.rem(place - step + line, line) * QUAD
+
+    def y_copy(step):
+        tok = line_source(step) + quad
+        src = kv_ref if step == 0 else cache.at[rows_of(tok)]
+        return remote(
+            src, cache.at[rows_of(tok)], y_send.at[step], y_recv.at[step], side
+        )
+
+    def s_copy(step, of_side):
+        tok = line_source(step) + (lax.rem(side, QUAD) if of_side else quad)
+        src = kv_ref if step == 0 and not of_side else cache.at[rows_of(tok)]
+        slot = step + (line if of_side else 0)
+        return remote(src, cache.at[rows_of(tok)], s_send.at[slot], s_recv.at[slot], sib)
+
+    def c_copy(step):
+        return remote(
+            column_ref,
+            column_tp.at[step],
+            c_send.at[step],
+            c_recv.at[step],
+            me,
+            lax.rem(tp + step, tp_count),
+        )
+
+    def a_copy(step):
+        return remote(
+            column_mid,
+            column_all.at[me],
+            a_send.at[step],
+            a_recv.at[step],
+            lax.rem(me + step, tok_count),
+        )
+
+    def o_copy(step):
+        return remote(
+            out_mine,
+            out_all.at[me],
+            o_send.at[step],
+            o_recv.at[step],
+            lax.rem(me + step, tok_count),
+        )
+
+    def each(copy, act):
+        def go(step, carry):
+            getattr(copy(step), act)()
+            return carry
+
+        lax.fori_loop(1, tok_count, go, 0)
+
+    meet_all(pltpu.get_barrier_semaphore(), me, tp, tok_count, tp_count)
+    for step in range(1, tp_count):
+        c_copy(step).start()
+    y_copy(0).start()
+    for step in range(1, line):
+        z_copy(step).start()
+    s_copy(0, False).start()
+    cache[rows_of(me)] = kv_ref[...]
+    joined = column_ref[...]
+    for step in range(1, tp_count):
+        c_copy(step).wait()
+        joined = jnp.maximum(joined, column_tp[step])
+    column_mid[...] = joined
+    column_all[me] = joined
+    for step in range(1, line):
+        z_copy(step).wait_recv()
+        y_copy(step).start()
+        s_copy(step, False).start()
+    each(a_copy, "start")
+    for step in range(line):
+        y_copy(step).wait_recv()
+        s_copy(step, True).start()
+    for step in range(line):
+        s_copy(step, False).wait_recv()
+        s_copy(step, True).wait_recv()
+
+    position = lax.broadcasted_iota(jnp.int32, (tok_dev, keys), 0) + me * tok_dev
+    allowed = (doc_mine_ref[...] == doc_all_ref[...]) & (
+        lax.broadcasted_iota(jnp.int32, (tok_dev, keys), 1) <= position
+    )
+    group = QHEADS // KVH
+    for kv in range(kv_here):
+        heads = [
+            slice((kv * group + g) * HEAD, (kv * group + g + 1) * HEAD)
+            for g in range(group)
+        ]
+        query = jnp.concatenate([query_ref[:, head] for head in heads], axis=0)
+        key = cache[:, kv * HEAD : (kv + 1) * HEAD]
+        value = cache[:, (kv_here + kv) * HEAD : (kv_here + kv + 1) * HEAD]
+        scores = lax.dot_general(
+            query, key, (((1,), (1,)), ((), ())), preferred_element_type=jnp.float32
+        ) * (1.0 / math.sqrt(HEAD))
+        scores = jnp.where(
+            allowed[None], scores.reshape(group, tok_dev, keys), -1e30
+        ).reshape(group * tok_dev, keys)
+        weights = jnp.exp(scores - jnp.max(scores, axis=1, keepdims=True))
+        totals = jnp.sum(weights, axis=1, keepdims=True)
+        mixed = jnp.dot(
+            weights.astype(jnp.bfloat16), value, preferred_element_type=jnp.float32
+        )
+        mixed = (mixed / totals).astype(jnp.bfloat16)
+        for g, head in enumerate(heads):
+            piece = mixed[g * tok_dev : (g + 1) * tok_dev]
+            out_ref[:, head] = piece
+            out_mine[:, head] = jnp.max(
+                jnp.abs(piece.astype(jnp.float32)), axis=0, keepdims=True
+            )
+    out_all[me] = out_mine[...]
+    each(o_copy, "start")
+    each(a_copy, "wait")
+    scale_ref[...] = jnp.maximum(jnp.max(column_all[...], axis=0), 1e-05) / 127.0
+    each(o_copy, "wait")
+    out_peak_ref[...] = jnp.max(out_all[...], axis=0)
+    for step in range(line):
+        if step > 0:
+            z_copy(step).wait_send()
+        y_copy(step).wait_send()
+        s_copy(step, False).wait_send()
+        s_copy(step, True).wait_send()
+
+
+def back(query, keys_values, doc_mine, doc_all, column_local):
+    tok_count, tp_count = lax.axis_size("tok"), lax.axis_size("tp")
+    line = tok_count // QUAD
+    tok_dev, width = query.shape
+    kv_here = keys_values.shape[1] // (2 * HEAD)
+    columns = column_local.shape[1]
+    vmem = pl.BlockSpec(memory_space=pltpu.VMEM)
+    dma = pltpu.SemaphoreType.DMA
+    f32 = jnp.float32
+    return pl.pallas_call(
+        functools.partial(back_kernel, line, tp_count, kv_here),
+        out_shape=(
+            jax.ShapeDtypeStruct((tok_dev, width), jnp.bfloat16),
+            jax.ShapeDtypeStruct((1, width), f32),
+            jax.ShapeDtypeStruct((1, columns), f32),
+        ),
+        in_specs=[vmem] * 5,
+        out_specs=(vmem,) * 3,
+        scratch_shapes=[
+            pltpu.VMEM((tok_dev * tok_count, keys_values.shape[1]), jnp.bfloat16),
+            pltpu.VMEM((tp_count, 1, columns), f32),
+            pltpu.VMEM((1, columns), f32),
+            pltpu.VMEM((tok_count, 1, columns), f32),
+            pltpu.VMEM((1, width), f32),
+            pltpu.VMEM((tok_count, 1, width), f32),
+        ]
+        + [dma((line,))] * 4
+        + [dma((2 * line,))] * 2
+        + [dma((tp_count,))] * 2
+        + [dma((tok_count,))] * 4,
+        compiler_params=pltpu.CompilerParams(
+            collective_id=1, has_side_effects=True, vmem_limit_bytes=60 * 1024 * 1024
+        ),
+    )(query, keys_values, doc_mine, doc_all, column_local)
 
 
 def on_device(hidden, norm_gain, w_query, w_key, w_value, doc_ids):
@@ -365,7 +642,6 @@
     tp_index = lax.axis_index("tp")
     heads_here = w_query.shape[1] // HEAD
     kv_here = w_key.shape[1] // HEAD
-    group_size = QHEADS // KVH
     matrices = (w_query, w_key, w_value)
     states = hidden.astype(jnp.float32)
     normed = (
@@ -373,20 +649,20 @@
         * lax.rsqrt(jnp.mean(states * states, axis=1, keepdims=True) + 1e-05)
         * norm_gain[None, :]
     ).astype(jnp.bfloat16)
-    summed, peaks, *relaid = front(normed, matrices)
+    lanes = -tok_dev % 128
+    doc_row = jnp.pad(doc_ids, (0, lanes))[None]
+    summed, peaks, docs, *relaid = front(normed, doc_row, matrices)
+    doc_all = docs[:, 0, :tok_dev].reshape(1, -1)
     query_columns, key_columns = w_query.shape[1], w_key.shape[1]
     projected = (
         summed[:, :query_columns],
         summed[:, query_columns : query_columns + key_columns],
         summed[:, query_columns + key_columns :],
     )
-    tok_count = lax.axis_size("tok")
-    quads = [[i + j for j in range(QUAD)] for i in range(0, tok_count, QUAD)]
-    quad_peak = lax.pmax(peaks[0], "tok", axis_index_groups=quads)
     sub_rows = row_count // tp_count
     smooth_part = smooth_from(
         lax.dynamic_slice_in_dim(
-            quad_peak, (tok_index % QUAD) * row_count + tp_index * sub_rows, sub_rows
+            peaks[0], (tok_index % QUAD) * row_count + tp_index * sub_rows, sub_rows
         ),
         functools.reduce(
             jnp.maximum, [jnp.max(jnp.abs(block), axis=1) for block in relaid]
@@ -398,20 +674,12 @@
             for block in relaid
         ]
     )
-    every = jnp.maximum(lax.pmax(column_local, ("tok", "tp")), 1e-05) / 127.0
-    every_scale = jnp.split(
-        every, [relaid[0].shape[1], relaid[0].shape[1] + relaid[1].shape[1]]
-    )
-    scales = tuple(
-        lax.dynamic_slice_in_dim(scale, tp_index * matrix.shape[1], matrix.shape[1])
-        for scale, matrix in zip(every_scale, matrices)
-    )
     query_positions = tok_index * tok_dev + jnp.arange(tok_dev, dtype=jnp.int32)
     positions = query_positions.astype(jnp.float32)
     query = (
         rotate(projected[0].reshape(tok_dev, heads_here, HEAD), positions)
         .astype(jnp.bfloat16)
-        .reshape(tok_dev, kv_here, group_size, HEAD)
+        .reshape(tok_dev, heads_here * HEAD)
     )
     key = (
         rotate(projected[1].reshape(tok_dev, kv_here, HEAD), positions)
@@ -419,43 +687,22 @@
         .reshape(tok_dev, kv_here * HEAD)
     )
     value = projected[2].astype(jnp.bfloat16)
-    score_scale = 1.0 / math.sqrt(HEAD)
-    highest = jnp.full((kv_here, group_size, tok_dev), -1e30, jnp.float32)
-    both = lax.all_gather(jnp.concatenate([key, value], axis=1), "tok", axis=0, tiled=True)
-    key_block, value_block = both[:, :key_columns], both[:, key_columns:]
-    doc_block = lax.all_gather(doc_ids, "tok", axis=0, tiled=True)
-    length = key_block.shape[0]
-    scores = (
-        jnp.einsum(
-            "tkgd,skd->kgts",
-            query,
-            key_block.reshape(length, kv_here, HEAD),
-            preferred_element_type=jnp.float32,
-        )
-        * score_scale
-    )
-    key_positions = jnp.arange(length, dtype=jnp.int32)
-    allowed = (doc_ids[:, None] == doc_block[None, :]) & (
-        key_positions[None, :] <= query_positions[:, None]
-    )
-    scores = jnp.where(allowed, scores, -1e30)
-    raised = jnp.maximum(highest, jnp.max(scores, axis=3))
-    weights = jnp.where(allowed, jnp.exp(scores - raised[..., None]), 0.0)
-    totals = jnp.sum(weights, axis=3)
-    accumulated = jnp.einsum(
-        "kgts,skd->kgtd",
-        weights.astype(jnp.bfloat16),
-        value_block.reshape(length, kv_here, HEAD),
-        preferred_element_type=jnp.float32,
-    )
-    highest, totals, accumulated = (raised, totals, accumulated)
-    attended = (
-        (accumulated / totals[..., None])
-        .transpose(2, 0, 1, 3)
-        .reshape(tok_dev, heads_here * HEAD)
-        .astype(jnp.bfloat16)
-    )
-    out_scale = lax.pmax(jnp.max(jnp.abs(attended), axis=0).astype(jnp.float32), "tok")
+    attended, out_scale, column_scales = back(
+        query,
+        jnp.concatenate([key, value], axis=1),
+        doc_ids[:, None],
+        doc_all,
+        column_local[None],
+    )
+    out_scale = out_scale[0]
+    every = column_scales[0]
+    every_scale = jnp.split(
+        every, [relaid[0].shape[1], relaid[0].shape[1] + relaid[1].shape[1]]
+    )
+    scales = tuple(
+        lax.dynamic_slice_in_dim(scale, tp_index * matrix.shape[1], matrix.shape[1])
+        for scale, matrix in zip(every_scale, matrices)
+    )
     gain_part = lax.dynamic_slice_in_dim(
         norm_gain, tok_index * row_count + tp_index * sub_rows, sub_rows
     )

time: 305 us -> 236 us (0.77)
  blocking collectives: 88.9 us -> 0 us
  Pallas kernels: 156 us -> 206 us
  between operations: 15 us -> 0.82 us
  matrix products: 9.25 us -> 0 us
  local copies, waits for them, and re-layouts: 15.5 us -> 11.9 us
  other arithmetic: 20 us -> 16.8 us
    pmax x3 -> x0, blocking collectives: 77.3 us -> none  [the longest x1 41 us: on_device(): every = jnp.maximum(lax.pmax(column_local, ('tok', 'tp')), 1e-05) / 127.0]
    pallas_call x0 -> x1, Pallas kernels: none -> 46.5 us  [back(): pl.pallas_call(functools.partial(back_kernel, line, tp_count, kv_here), o...]
    unnamed x1 -> x0, blocking collectives: 11.6 us -> none
    dot_general x2 -> x0, matrix products: 9.25 us -> none  [the longest x1 6.76 us: on_device(): jnp.einsum('tkgd,skd->kgts', query, key_block.reshape(length, kv_here, HE...]
    reduce_sum x1 -> x0, other arithmetic: 6.05 us -> none  [on_device(): totals = jnp.sum(weights, axis=3)]
    pallas_call x1, Pallas kernels: 156 us -> 159 us  [front(): pl.pallas_call(functools.partial(front_kernel, chunks, line, tp_count), o...]
    slice x1, local copies, waits for them, and re-layouts: 3.22 us -> 0.02 us  [on_device(): doc_all = docs[:, 0, :tok_dev].reshape(1, -1)]
  transfers between devices with their start and end apart: 1 -> 0, of which waited for: 0 -> 0; matrix products, arithmetic and copies ran while one was open for 4% -> 0% of each run, Pallas kernels for 0% -> 0%
where the time goes in v3:
time: 236 us; the launch traced here: 235 us
  Pallas kernels  206 us (87%)
  other arithmetic  16.8 us (7%)
  local copies, waits for them, and re-layouts  11.9 us (5%)
    pallas_call x1, Pallas kernels, front(): pl.pallas_call(functools.partial(front_kernel, chunks, line, tp_count), o...  159 us
    pallas_call x1, Pallas kernels, back(): pl.pallas_call(functools.partial(back_kernel, line, tp_count, kv_here), o...  46.5 us

profile of v3, /device:TPU:0, one launch (start us, length us, event | category | flops | bytes accessed | tf_op | source)
XLA Modules:
  0.0 235.3 jit_solution(10030860222799699962)
XLA Ops:
  0.7 1.8 fusion.1
  2.5 3.0 %fusion.3.normed_ref = bf16[96,8192]{1,0:T(8,128)(2,1)} fusion(bf16[96,8192]{1,0:T(8,128)(2,1)} %param.6, f32[8192]{0:T(1024)} %param.7, f32[96]{0:T(128)S(1)} %add_rsqrt_fusion), kind=kLoop, calls=%fused_computation.7 | loop fusion | flops 3145728 | bytes 3178880 | tf_op jit(solution)/shard_map/convert_element_type | solution.py:651
  6.0 159.3 %shard_map.133 = (f32[96,3072]{1,0:T(8,128)}, f32[1,2048]{1,0:T(1,128)}, s32[16,1,128]{2,1,0:T(1,128)}, bf16[256,4096]{1,0:T(8,128)(2,1)}, bf16[256,1024]{1,0:T(8,128)(2,1)}, /*index=5*/bf16[256,1024]{1,0:T(8,128)(2,1)}) custom-call(bf16[96,8192]{1,0:T(8,128)(2,1)} %fusion.3.normed_ref, s32[1,128]{1,0:T(1,128)} %pad_bitcast_fusion.doc_ref, ...), custom_call_target="tpu_custom_call" | custom-call | tf_op jit(solution)/shard_map/pallas_call | solution.py:372
  165.3 1.2 slice_bitcast_fusion
  166.9 0.6 copy-done.3
  168.2 0.8 copy.21
  169.0 1.6 slice.52
  170.6 0.9 slice.31
  171.6 1.0 subtract_convert_fusion.1
  172.8 1.6 pad_maximum_fusion.1.kv_ref
  174.4 0.7 copy.15.doc_mine_ref
  175.1 0.7 reshape_squeeze.3.doc_all_ref
  175.8 0.6 maximum_sqrt_fusion
  177.2 1.3 dynamic-slice_divide_fusion
  179.3 0.6 pad_maximum_fusion.3
  179.9 46.5 %shard_map.134 = (bf16[96,2048]{1,0:T(8,128)(2,1)}, f32[1,2048]{1,0:T(1,128)}, f32[1,6144]{1,0:T(1,128)}) custom-call(bf16[96,2048]{1,0:T(8,128)(2,1)} %bitcast.24, bf16[96,1024]{1,0:T(8,128)(2,1)} %pad_maximum_fusion.1.kv_ref, s32[96,1]{1,0:T(8,128)} %copy.15.doc_mine_ref, s32[1,1536]{1,0:T(1,128)} %reshape_squeeze.3.doc_all_ref, f32[1,6144]{1,0:T(1,128)} %bitcast.29), custom_call_target="tpu_custom_call" | custom-call | tf_op jit(solution)/shard_map/pallas_call | solution.py:610
  226.5 0.7 split.9
  227.2 2.7 %fusion = f32[256,4096]{1,0:T(8,128)} fusion(bf16[256,4096]{1,0:T(8,128)(2,1)S(1)} %copy-done, f32[4096]{0:T(1024)S(1)} %bitcast.28, f32[256]{0:T(256)S(1)} %get-tuple-element.30), kind=kLoop, calls=%fused_computation.2 | loop fusion | flops 3145728 | bytes 6308864 | tf_op jit(solution)/shard_map/div | solution.py:712
  229.9 0.7 fusion.6
  230.6 1.6 fusion.4
  232.2 0.6 constant_dynamic-slice_fusion.2
  232.8 0.6 constant_dynamic-slice_fusion.1
  234.0 0.7 copy.25
  234.7 0.6 copy.26
  (34 shorter events, 3.9 us)
Async XLA Ops:
  0.6 4.9 %copy-start.8 = (s32[96]{0:T(128)S(1)}, s32[96]{0:T(128)}, u32[]{:S(2)}) copy-start(s32[96]{0:T(128)} %param.11) | copy-start | bytes 1156
  166.9 0.6 copy-start.3
  166.9 0.6 copy-start.4
  167.6 7.6 %copy-start.6 = (s32[16,1,128]{2,1,0:T(1,128)S(1)}, s32[16,1,128]{2,1,0:T(1,128)}, u32[]{:S(2)}) copy-start(s32[16,1,128]{2,1,0:T(1,128)} %get-tuple-element.19) | copy-start | bytes 24580
  167.6 8.9 %copy-start.1 = (bf16[256,1024]{1,0:T(8,128)(2,1)S(1)}, bf16[256,1024]{1,0:T(8,128)(2,1)}, u32[]{:S(2)}) copy-start(bf16[256,1024]{1,0:T(8,128)(2,1)} %get-tuple-element.22) | copy-start | bytes 1572868
  167.6 8.9 %copy-start.2 = (bf16[256,1024]{1,0:T(8,128)(2,1)S(1)}, bf16[256,1024]{1,0:T(8,128)(2,1)}, u32[]{:S(2)}) copy-start(bf16[256,1024]{1,0:T(8,128)(2,1)} %get-tuple-element.23) | copy-start | bytes 1572868
  167.9 8.8 %copy-start = (bf16[256,4096]{1,0:T(8,128)(2,1)S(1)}, bf16[256,4096]{1,0:T(8,128)(2,1)}, u32[]{:S(2)}) copy-start(bf16[256,4096]{1,0:T(8,128)(2,1)} %get-tuple-element.21) | copy-start | bytes 6291460
  229.9 4.1 %copy-start.5 = (bf16[96,2048]{1,0:T(8,128)(2,1)S(1)}, bf16[96,2048]{1,0:T(8,128)(2,1)}, u32[]{:S(2)}) copy-start(bf16[96,2048]{1,0:T(8,128)(2,1)} %get-tuple-element.52) | copy-start | bytes 1179652
  229.9 4.8 %copy-start.7 = (f32[1,2048]{1,0:T(1,128)S(1)}, f32[1,2048]{1,0:T(1,128)}, u32[]{:S(2)}) copy-start(f32[1,2048]{1,0:T(1,128)} %get-tuple-element.25) | copy-start | bytes 24580

commit v4 on v3

--- a/solution.py
+++ b/solution.py
@@ -13,18 +13,16 @@
 QHEADS = 32
 
 
-def rotate(states, positions):
-    half = states.shape[-1] // 2
+def rotation(positions):
+    half = HEAD // 2
     inverse = jnp.exp(
-        jnp.arange(half, dtype=jnp.float32) * (-2.0 * math.log(10000.0) / states.shape[-1])
+        jnp.arange(half, dtype=jnp.float32) * (-2.0 * math.log(10000.0) / HEAD)
     )
     angles = positions[:, None] * inverse[None, :]
-    cosine = jnp.cos(angles)[:, None, :]
-    sine = jnp.sin(angles)[:, None, :]
-    first = states[..., :half]
-    second = states[..., half:]
-    return jnp.concatenate(
-        [first * cosine - second * sine, second * cosine + first * sine], axis=-1
+    cosine, sine = jnp.cos(angles), jnp.sin(angles)
+    return (
+        jnp.concatenate([cosine, cosine], axis=1),
+        jnp.concatenate([-sine, sine], axis=1),
     )
 
 
@@ -61,12 +59,16 @@
     chunks,
     line,
     tp_count,
+    share,
     normed_ref,
     doc_ref,
+    cosine_ref,
+    sine_ref,
     wq_ref,
     wk_ref,
     wv_ref,
-    sum_ref,
+    query_ref,
+    kv_ref,
     peak_ref,
     docs_ref,
     rq_ref,
@@ -85,6 +87,8 @@
     w_recv,
     t_send,
     t_recv,
+    m_send,
+    m_recv,
     x_send,
     x_recv,
     x_local,
@@ -139,16 +143,29 @@
             side if kind == 1 else sib,
         )
 
+    part = tok_dev // share
+    piece = lax.rem(tp, share)
+    mate = tp + 1 - 2 * piece
+
     def t_copy(step):
         to = lax.rem(place + step, line)
         width = QUAD * rows
-        return remote(
-            normed_ref.at[:, pl.ds(pl.multiple_of(to * width, 128), width)],
-            tokens.at[pl.ds(pl.multiple_of(place * tok_dev, 16), tok_dev)],
+        first = pl.multiple_of(piece * part, 16)
+        return remote(
+            normed_ref.at[
+                pl.ds(first, part), pl.ds(pl.multiple_of(to * width, 128), width)
+            ],
+            tokens.at[pl.ds(pl.multiple_of(place * tok_dev + first, 16), part)],
             t_send.at[step],
             t_recv.at[step],
             to * QUAD + quad,
         )
+
+    def m_copy(step):
+        source = lax.rem(place - step + line, line)
+        first = pl.multiple_of(source * tok_dev + piece * part, 16)
+        got = tokens.at[pl.ds(first, part)]
+        return remote(got, got, m_send.at[step], m_recv.at[step], me, mate)
 
     def x_copy(which, step):
         to = lax.rem(tp + step, tp_count)
@@ -190,16 +207,20 @@
     for c in range(len(chunks)):
         w_copy(1, c).start()
         w_copy(0, c).start()
-    for which in range(3):
-        for step in range(tp_count):
-            x_copy(which, step).start()
-
     width = QUAD * rows
     tokens[pl.ds(pl.multiple_of(place * tok_dev, 16), tok_dev)] = normed_ref[
         :, pl.ds(pl.multiple_of(place * width, 128), width)
     ]
     for step in range(1, line):
         t_copy(step).wait_recv()
+        if share == 2:
+            m_copy(step).start()
+    for which in range(3):
+        for step in range(tp_count):
+            x_copy(which, step).start()
+    if share == 2:
+        for step in range(1, line):
+            m_copy(step).wait_recv()
     mine[...] = jnp.max(
         jnp.abs(tokens[...].astype(jnp.float32)), axis=0, keepdims=True
     )
@@ -279,6 +300,7 @@
 
         lax.fori_loop(0, line, go, 0)
 
+    def finish(c):
         @pl.when(place > 0)
         def _():
             add_left(c, place)
@@ -287,7 +309,18 @@
         def _():
             add_right(c, place)
 
-        sum_ref[:, span(c)] = partial[block(place), span(c)]
+        which, start, size = chunks[c]
+        for head in range(size // HEAD):
+            base = span(c).start + head * HEAD
+            states = partial[block(place), base : base + HEAD]
+            if which < 2:
+                states = (
+                    states * cosine_ref[...]
+                    + pltpu.roll(states, HEAD // 2, 1) * sine_ref[...]
+                )
+            at = start + head * HEAD + (wk_ref.shape[1] if which == 2 else 0)
+            target = query_ref if which == 0 else kv_ref
+            target[:, at : at + HEAD] = states.astype(jnp.bfloat16)
 
     def columns_of(tok):
         return pl.ds(pl.multiple_of(lax.rem(tok, QUAD) * rows, 128), rows)
@@ -327,6 +360,8 @@
         if c > 0:
             reduce(c - 1)
     reduce(len(chunks) - 1)
+    for c in range(len(chunks)):
+        finish(c)
 
     for kind in range(3):
         p_copy(kind).wait()
@@ -336,6 +371,8 @@
     lax.fori_loop(1, line * QUAD, d_wait, 0)
     for step in range(1, line):
         t_copy(step).wait_send()
+        if share == 2:
+            m_copy(step).wait_send()
     for c in range(len(chunks)):
         for kind in range(3):
             w_copy(kind, c).wait_send()
@@ -359,7 +396,7 @@
             x_copy(which, step).wait_recv()
 
 
-def front(normed, doc_row, matrices):
+def front(normed, doc_row, cosine, sine, matrices):
     tok_count, tp_count = lax.axis_size("tok"), lax.axis_size("tp")
     line = tok_count // QUAD
     tok_dev = normed.shape[0]
@@ -367,12 +404,14 @@
     widths = [matrix.shape[1] for matrix in matrices]
     chunks = column_chunks(widths)
     total = sum(widths)
+    share = 2 if tp_count % 2 == 0 and tok_dev % 32 == 0 else 1
     vmem = pl.BlockSpec(memory_space=pltpu.VMEM)
     dma = pltpu.SemaphoreType.DMA
     return pl.pallas_call(
-        functools.partial(front_kernel, chunks, line, tp_count),
+        functools.partial(front_kernel, chunks, line, tp_count, share),
         out_shape=(
-            jax.ShapeDtypeStruct((tok_dev, total), jnp.float32),
+            jax.ShapeDtypeStruct((tok_dev, widths[0]), jnp.bfloat16),
+            jax.ShapeDtypeStruct((tok_dev, widths[1] + widths[2]), jnp.bfloat16),
             jax.ShapeDtypeStruct((1, QUAD * rows), jnp.float32),
             jax.ShapeDtypeStruct((tok_count,) + doc_row.shape, jnp.int32),
         )
@@ -380,8 +419,8 @@
             jax.ShapeDtypeStruct((rows // tp_count, width * tp_count), jnp.bfloat16)
             for width in widths
         ),
-        in_specs=[vmem] * 5,
-        out_specs=(vmem, vmem, vmem) + (pl.BlockSpec(memory_space=pl.ANY),) * 3,
+        in_specs=[vmem] * 7,
+        out_specs=(vmem,) * 4 + (pl.BlockSpec(memory_space=pl.ANY),) * 3,
         scratch_shapes=[
             pltpu.VMEM((1, QUAD * rows), jnp.float32),
             pltpu.VMEM((3, 1, QUAD * rows), jnp.float32),
@@ -396,6 +435,8 @@
             pltpu.VMEM((line * tok_dev, total), jnp.float32),
             dma((3, len(chunks))),
             dma((3, len(chunks))),
+            dma((line,)),
+            dma((line,)),
             dma((line,)),
             dma((line,)),
             dma((3, tp_count)),
@@ -413,7 +454,7 @@
         compiler_params=pltpu.CompilerParams(
             collective_id=0, has_side_effects=True, vmem_limit_bytes=60 * 1024 * 1024
         ),
-    )(normed, doc_row, *matrices)
+    )(normed, doc_row, cosine, sine, *matrices)
 
 
 def back_kernel(
@@ -640,8 +681,6 @@
     tp_count = lax.axis_size("tp")
     tok_index = lax.axis_index("tok")
     tp_index = lax.axis_index("tp")
-    heads_here = w_query.shape[1] // HEAD
-    kv_here = w_key.shape[1] // HEAD
     matrices = (w_query, w_key, w_value)
     states = hidden.astype(jnp.float32)
     normed = (
@@ -651,14 +690,13 @@
     ).astype(jnp.bfloat16)
     lanes = -tok_dev % 128
     doc_row = jnp.pad(doc_ids, (0, lanes))[None]
-    summed, peaks, docs, *relaid = front(normed, doc_row, matrices)
+    positions = (tok_index * tok_dev + jnp.arange(tok_dev, dtype=jnp.int32)).astype(
+        jnp.float32
+    )
+    query, keys_values, peaks, docs, *relaid = front(
+        normed, doc_row, *rotation(positions), matrices
+    )
     doc_all = docs[:, 0, :tok_dev].reshape(1, -1)
-    query_columns, key_columns = w_query.shape[1], w_key.shape[1]
-    projected = (
-        summed[:, :query_columns],
-        summed[:, query_columns : query_columns + key_columns],
-        summed[:, query_columns + key_columns :],
-    )
     sub_rows = row_count // tp_count
     smooth_part = smooth_from(
         lax.dynamic_slice_in_dim(
@@ -674,22 +712,9 @@
             for block in relaid
         ]
     )
-    query_positions = tok_index * tok_dev + jnp.arange(tok_dev, dtype=jnp.int32)
-    positions = query_positions.astype(jnp.float32)
-    query = (
-        rotate(projected[0].reshape(tok_dev, heads_here, HEAD), positions)
-        .astype(jnp.bfloat16)
-        .reshape(tok_dev, heads_here * HEAD)
-    )
-    key = (
-        rotate(projected[1].reshape(tok_dev, kv_here, HEAD), positions)
-        .astype(jnp.bfloat16)
-        .reshape(tok_dev, kv_here * HEAD)
-    )
-    value = projected[2].astype(jnp.bfloat16)
     attended, out_scale, column_scales = back(
         query,
-        jnp.concatenate([key, value], axis=1),
+        keys_values,
         doc_ids[:, None],
         doc_all,
         column_local[None],

time: 236 us -> 215 us (0.911)
  Pallas kernels: 206 us -> 188 us
  local copies, waits for them, and re-layouts: 11.9 us -> 7.41 us
    pallas_call x1, Pallas kernels: 159 us -> 142 us  [front(): pl.pallas_call(functools.partial(front_kernel, chunks, line, tp_count, sh...]
    reduce_max x2 -> x3, other arithmetic: 0.74 us -> 4.5 us  [on_device(): jnp.max(jnp.abs(block), axis=1)]
    unnamed x24 -> x14, local copies, waits for them, and re-layouts: 4.19 us -> 1.37 us
    slice x2 -> x0, local copies, waits for them, and re-layouts: 2.52 us -> none  [the longest x1 1.58 us: on_device(): summed[:, query_columns + key_columns:]]
where the time goes in v4:
time: 215 us; the launch traced here: 214 us
  Pallas kernels  188 us (87%)
  other arithmetic  18 us (8%)
  local copies, waits for them, and re-layouts  7.41 us (3%)
    pallas_call x1, Pallas kernels, front(): pl.pallas_call(functools.partial(front_kernel, chunks, line, tp_count, sh...  142 us
    pallas_call x1, Pallas kernels, back(): pl.pallas_call(functools.partial(back_kernel, line, tp_count, kv_here), o...  46.6 us
    reduce_max x3, other arithmetic, on_device(): jnp.max(jnp.abs(block), axis=1)  4.5 us
    div x2, other arithmetic, on_device(): smooth_part[:, None] * block.astype(jnp.float32) / column_scale[None, :]  4.31 us

profile of v4, /device:TPU:0, one launch (start us, length us, event | category | flops | bytes accessed | tf_op | source)
XLA Modules:
  0.0 214.4 jit_solution(18400498866735299392)
XLA Ops:
  0.7 1.8 fusion.1
  2.5 3.0 %fusion.3.normed_ref = bf16[96,8192]{1,0:T(8,128)(2,1)} fusion(bf16[96,8192]{1,0:T(8,128)(2,1)} %param.6, f32[8192]{0:T(1024)} %param.7, f32[96]{0:T(128)S(1)} %add_rsqrt_fusion), kind=kLoop, calls=%fused_computation.7 | loop fusion | flops 3145728 | bytes 3178880 | tf_op jit(solution)/shard_map/convert_element_type | solution.py:690
  5.5 0.5 pad_bitcast_fusion.doc_ref
  6.3 0.7 pad_maximum_fusion
  7.0 141.6 %shard_map.133 = (bf16[96,2048]{1,0:T(8,128)(2,1)}, bf16[96,1024]{1,0:T(8,128)(2,1)}, f32[1,2048]{1,0:T(1,128)}, s32[16,1,128]{2,1,0:T(1,128)}, bf16[256,4096]{1...) custom-call(bf16[96,8192]{1,0:T(8,128)(2,1)} %fusion.3.normed_ref, ...), custom_call_target="tpu_custom_call" | custom-call | tf_op jit(solution)/shard_map/pallas_call | solution.py:410
  148.7 0.7 copy.15.doc_mine_ref
  149.4 0.9 slice_reduce_fusion
  150.3 0.7 reshape_squeeze.3.doc_all_ref
  151.0 0.7 maximum_sqrt_fusion
  151.7 1.2 abs_reduce_fusion.4
  152.9 2.1 abs_reduce_fusion.1
  154.9 1.2 abs_reduce_fusion.5
  156.2 1.3 dynamic-slice_divide_fusion
  158.3 0.6 pad_maximum_fusion.2
  158.9 46.6 %shard_map.134 = (bf16[96,2048]{1,0:T(8,128)(2,1)}, f32[1,2048]{1,0:T(1,128)}, f32[1,6144]{1,0:T(1,128)}) custom-call(bf16[96,2048]{1,0:T(8,128)(2,1)} %get-tuple-element.19.query_ref, bf16[96,1024]{1,0:T(8,128)(2,1)} %get-tuple-element.20.kv_ref, s32[96,1]{1,0:T(8,128)} %copy.15.doc_mine_ref, s32[1,1536]{1,0:T(1,128)} %reshape_squeeze.3.doc_all_ref, ...), custom_call_target="tpu_custom_call" | custom-call | tf_op jit(solution)/shard_map/pallas_call | solution.py:651
  205.5 0.7 split.9
  206.2 2.7 %fusion = f32[256,4096]{1,0:T(8,128)} fusion(bf16[256,4096]{1,0:T(8,128)(2,1)S(1)} %copy-done, f32[4096]{0:T(1024)S(1)} %bitcast.12, f32[256]{0:T(256)S(1)} %get-tuple-element.32), kind=kLoop, calls=%fused_computation.2 | loop fusion | flops 3145728 | bytes 6308864 | tf_op jit(solution)/shard_map/div | solution.py:737
  208.9 0.7 fusion.7
  209.7 1.6 fusion.4
  211.2 0.6 constant_dynamic-slice_fusion.2
  211.8 0.6 constant_dynamic-slice_fusion.1
  212.4 0.6 constant_dynamic-slice_fusion
  213.0 0.7 copy.18
  213.8 0.6 copy.19
  (18 shorter events, 1.1 us)
Async XLA Ops:
  0.6 4.9 %copy-start.5 = (s32[96]{0:T(128)S(1)}, s32[96]{0:T(128)}, u32[]{:S(2)}) copy-start(s32[96]{0:T(128)} %param.11) | copy-start | bytes 1156
  148.6 8.9 %copy-start.1 = (bf16[256,1024]{1,0:T(8,128)(2,1)S(1)}, bf16[256,1024]{1,0:T(8,128)(2,1)}, u32[]{:S(2)}) copy-start(bf16[256,1024]{1,0:T(8,128)(2,1)} %get-tuple-element.24) | copy-start | bytes 1572868
  148.6 8.9 %copy-start.2 = (bf16[256,1024]{1,0:T(8,128)(2,1)S(1)}, bf16[256,1024]{1,0:T(8,128)(2,1)}, u32[]{:S(2)}) copy-start(bf16[256,1024]{1,0:T(8,128)(2,1)} %get-tuple-element.25) | copy-start | bytes 1572868
  148.6 9.2 %copy-start = (bf16[256,4096]{1,0:T(8,128)(2,1)S(1)}, bf16[256,4096]{1,0:T(8,128)(2,1)}, u32[]{:S(2)}) copy-start(bf16[256,4096]{1,0:T(8,128)(2,1)} %get-tuple-element.23) | copy-start | bytes 6291460
  208.9 4.1 %copy-start.3 = (bf16[96,2048]{1,0:T(8,128)(2,1)S(1)}, bf16[96,2048]{1,0:T(8,128)(2,1)}, u32[]{:S(2)}) copy-start(bf16[96,2048]{1,0:T(8,128)(2,1)} %get-tuple-element.51) | copy-start | bytes 1179652
  208.9 4.8 %copy-start.4 = (f32[1,2048]{1,0:T(1,128)S(1)}, f32[1,2048]{1,0:T(1,128)}, u32[]{:S(2)}) copy-start(f32[1,2048]{1,0:T(1,128)} %get-tuple-element.27) | copy-start | bytes 24580
